TPU v7x, 128 devices: a whole 4x4x4 slice. The times are simulated.
128 devices in a mesh: model: 16 (over z, y), data: 8 (over x, core).
Axes of the slice: x: 4, y: 4, z: 4, core: 2. Of those that a mesh axis runs over, the one named last changes fastest.
Arguments:
- x_tokens: bfloat16 [16384, 2048], P('data')
- dy_tokens: bfloat16 [16384, 2048], P('data')
- w_col: bfloat16 [2, 2048, 2048], P(None, None, 'model')
- w_row: bfloat16 [2, 2048, 2048], P(None, 'model')
- a_old_col: float32 [2, 2048, 2048], replicated
- s_old_col: float32 [2, 2048, 128], P(None, 'model')
- a_old_row: float32 [2, 2048, 128], P(None, 'model')
- s_old_row: float32 [2, 2048, 2048], replicated
- a_inv_col: float32 [2, 2048, 2048], replicated
- s_inv_col: float32 [2, 2048, 128], P(None, 'model')
- a_inv_row: float32 [2, 2048, 128], P(None, 'model')
- s_inv_row: float32 [2, 2048, 2048], replicated
Outputs:
- output 1: float32 [2, 2048, 2048], P(None, None, 'model')
- output 2: float32 [2, 2048, 2048], P(None, 'model')
- output 3: float32 [2, 2048, 2048], replicated
- output 4: float32 [2, 2048, 128], P(None, 'model')
- output 5: float32 [2, 2048, 128], P(None, 'model')
- output 6: float32 [2, 2048, 2048], replicated
All inputs are finite; a program needn't handle non-finite values.
Results may differ from a plain program's by a relative error of at most 0.0075489.
Values are sent between devices in bfloat16 or wider.
A program may use at most 1 GiB of HBM per device.

v0:
```python
import math
import jax
import jax.numpy as jnp
from jax import lax
from jax.sharding import PartitionSpec as P

FACTOR_DECAY = 0.8
GELU_SCALE = math.sqrt(2.0 / math.pi)
GELU_CUBIC = 0.044715
EXACT = lax.Precision.HIGHEST
TN_DIMS = (((0,), (0,)), ((), ()))
NT_DIMS = (((1,), (1,)), ((), ()))


def gelu_value(pre_act):
    tanh_arg = GELU_SCALE * (pre_act + GELU_CUBIC * pre_act * pre_act * pre_act)
    return 0.5 * pre_act * (1.0 + jnp.tanh(tanh_arg))


def gelu_slope(pre_act):
    tanh_arg = GELU_SCALE * (pre_act + GELU_CUBIC * pre_act * pre_act * pre_act)
    tanh_val = jnp.tanh(tanh_arg)
    return 0.5 * (1.0 + tanh_val) + 0.5 * pre_act * (1.0 - tanh_val * tanh_val) * GELU_SCALE * (1.0 + 3.0 * GELU_CUBIC * pre_act * pre_act)


def activate(pre_act):
    return gelu_value(pre_act.astype(jnp.float32)).astype(jnp.bfloat16)


def back_gate(grad_act, pre_act):
    return (grad_act.astype(jnp.float32) * gelu_slope(pre_act.astype(jnp.float32))).astype(jnp.bfloat16)


def matmul(left_mat, right_mat):
    return jnp.dot(left_mat, right_mat, preferred_element_type=jnp.float32)


def matmul_tn(left_mat, right_mat):
    return lax.dot_general(left_mat, right_mat, TN_DIMS, preferred_element_type=jnp.float32)


def matmul_nt(left_mat, right_mat):
    return lax.dot_general(left_mat, right_mat, NT_DIMS, preferred_element_type=jnp.float32)


def exact_dot(left_mat, right_mat):
    return jnp.dot(left_mat, right_mat, precision=EXACT, preferred_element_type=jnp.float32)


def precondition(a_inv, grad_mat, s_inv):
    return exact_dot(exact_dot(a_inv, grad_mat), s_inv)


def blend_factor(old_mats, first_new, second_new, inv_rows):
    return FACTOR_DECAY * old_mats + (1.0 - FACTOR_DECAY) * inv_rows * jnp.stack([first_new, second_new])


def local_pass(x_tokens, dy_tokens, w_col, w_row):
    z_one = matmul(x_tokens, w_col[0]).astype(jnp.bfloat16)
    h_one = activate(z_one)
    z_two = lax.psum(matmul(h_one, w_row[0]), 'model').astype(jnp.bfloat16)
    h_two = activate(z_two)
    z_three = matmul(h_two, w_col[1]).astype(jnp.bfloat16)
    h_three = activate(z_three)
    g_three = back_gate(matmul_nt(dy_tokens, w_row[1]).astype(jnp.bfloat16), z_three)
    dh_two = lax.psum(matmul_nt(g_three, w_col[1]), 'model').astype(jnp.bfloat16)
    g_two = back_gate(dh_two, z_two)
    g_one = back_gate(matmul_nt(g_two, w_row[0]).astype(jnp.bfloat16), z_one)
    return [x_tokens, h_one, h_two, h_three], [g_one, g_two, g_three, dy_tokens]


def finish_step(totals, inv_rows, a_old_col, s_old_col, a_old_row, s_old_row, a_inv_col, s_inv_col, a_inv_row, s_inv_row):
    weight_grads = [total_mat * inv_rows for total_mat in totals[8:]]
    u_col = jnp.stack([precondition(a_inv_col[0], weight_grads[0], s_inv_col[0]), precondition(a_inv_col[1], weight_grads[2], s_inv_col[1])])
    u_row = jnp.stack([precondition(a_inv_row[0], weight_grads[1], s_inv_row[0]), precondition(a_inv_row[1], weight_grads[3], s_inv_row[1])])
    a_new_col = blend_factor(a_old_col, totals[0], totals[2], inv_rows)
    s_new_col = blend_factor(s_old_col, totals[4], totals[6], inv_rows)
    a_new_row = blend_factor(a_old_row, totals[1], totals[3], inv_rows)
    s_new_row = blend_factor(s_old_row, totals[5], totals[7], inv_rows)
    return (u_col, u_row, a_new_col, s_new_col, a_new_row, s_new_row)


def solution(mesh):
    data_ways = mesh.shape['data']

    def shard_body(x_tokens, dy_tokens, w_col, w_row, a_old_col, s_old_col, a_old_row, s_old_row, a_inv_col, s_inv_col, a_inv_row, s_inv_row):
        layer_in, layer_grad = local_pass(x_tokens, dy_tokens, w_col, w_row)
        local_sums = [matmul_tn(layer_in[layer], layer_in[layer]) for layer in range(4)]
        local_sums += [matmul_tn(layer_grad[layer], layer_grad[layer]) for layer in range(4)]
        local_sums += [matmul_tn(layer_in[layer], layer_grad[layer]) for layer in range(4)]
        totals = lax.psum(local_sums, 'data')
        inv_rows = 1.0 / (x_tokens.shape[0] * data_ways)
        return finish_step(totals, inv_rows, a_old_col, s_old_col, a_old_row, s_old_row, a_inv_col, s_inv_col, a_inv_row, s_inv_row)

    batch_split = P('data', None)
    col_split = P(None, None, 'model')
    row_split = P(None, 'model', None)
    replicated = P()
    return jax.shard_map(
        shard_body,
        mesh=mesh,
        in_specs=(batch_split, batch_split, col_split, row_split, replicated, row_split, row_split, replicated, replicated, row_split, row_split, replicated),
        out_specs=(col_split, row_split, replicated, row_split, row_split, replicated),
        check_vma=False,
    )
```

profile of v0, /device:TPU:1, one launch (start us, length us, event | category | flops | bytes accessed | tf_op | source)
XLA Modules:
  0.0 1743.7 jit_solution(4217818468687047850)
XLA Ops:
  7.2 0.0 all-reduce.5.cloned.1.call-start
  7.2 5.8 convolution_convert_fusion.2
  13.0 1.5 convolution_bitcast_fusion.8
  14.5 9.6 fusion.65
  24.1 365.5 %all-reduce.6 = bf16[2048,2048]{1,0:T(8,128)(2,1)} all-reduce(f32[2048,2048]{1,0:T(8,128)} %fusion.65), channel_id=1, replica_groups=mesh['model'=16,'data'=8] {'model'}, use_global_device_ids=true, to_apply=%region_0.0 | all-reduce | flops 4194304 | bytes 25165824 | tf_op jit(solution)/shard_map/psum | solution.py:61
  389.6 7.6 fusion.4
  397.2 0.0 copy-done.3
  397.2 0.0 slice-start.2
  397.2 2.4 convolution_convert_fusion.1
  399.6 1.5 convolution_bitcast_fusion.7
  401.1 0.0 copy-done.4
  401.1 6.2 fusion.35
  407.4 0.0 slice-done.2
  407.4 0.0 slice-done.3
  407.4 2.5 fusion.94
  409.9 1.0 convolution_bitcast_fusion.9
  410.9 2.3 fusion.100
  413.2 21.2 %convolution_bitcast_fusion.2 = f32[1,2048,2048]{2,1,0:T(8,128)} fusion(bf16[2048,2048]{1,0:T(8,128)(2,1)S(1)} %fusion.4), kind=kOutput, calls=%fused_computation.36 | convolution fusion | flops 17179869184 | bytes 25165824 | tf_op jit(solution)/shard_map/dot_general | solution.py:39
  434.4 8.5 fusion.61
  442.9 359.6 %all-reduce.7 = bf16[2048,2048]{1,0:T(8,128)(2,1)} all-reduce(f32[2048,2048]{1,0:T(8,128)} %fusion.61), channel_id=1, replica_groups=mesh['model'=16,'data'=8] {'model'}, use_global_device_ids=true, to_apply=%region_1.0 | all-reduce | flops 4194304 | bytes 25165824 | tf_op jit(solution)/shard_map/psum | solution.py:66
  802.5 13.9 fusion.9
  816.5 2.8 fusion.36
  819.3 1.0 convolution_bitcast_fusion.10
  820.2 5.6 convolution_bitcast_fusion.4
  825.9 2.5 fusion.97
  828.4 21.5 %convolution_bitcast_fusion.1 = f32[1,2048,2048]{2,1,0:T(8,128)} fusion(bf16[2048,2048]{1,0:T(8,128)(2,1)S(1)} %fusion.9), kind=kOutput, calls=%fused_computation.35 | convolution fusion | flops 17179869184 | bytes 25165824 | tf_op jit(solution)/shard_map/dot_general | solution.py:39
  849.8 0.0 slice-done
  849.8 0.0 slice-done.1
  849.8 21.0 %convolution_bitcast_fusion.3 = f32[1,2048,2048]{2,1,0:T(8,128)} fusion(bf16[2048,2048]{1,0:T(8,128)(2,1)S(1)} %bitcast.98), kind=kOutput, calls=%fused_computation.37 | convolution fusion | flops 17179869184 | bytes 25165824 | tf_op jit(solution)/shard_map/dot_general | solution.py:39
  870.9 0.0 slice-done.4
  870.9 0.0 slice-done.5
  870.9 21.2 %convolution_bitcast_fusion = f32[1,2048,2048]{2,1,0:T(8,128)} fusion(bf16[2048,2048]{1,0:T(8,128)(2,1)S(1)} %bitcast.102), kind=kOutput, calls=%fused_computation.34 | convolution fusion | flops 17179869184 | bytes 25165824 | tf_op jit(solution)/shard_map/dot_general | solution.py:39
  892.1 0.0 all-reduce.5.cloned.1.call-update
  892.1 700.0 %all-reduce.5.cloned.1.call-done = (f32[2048,128]{0,1:T(8,128)}, f32[2048,128]{0,1:T(8,128)}, f32[128,2048]{1,0:T(8,128)}, f32[128,2048]{1,0:T(8,128)}, f32[1,20...) async-done(((f32[2048,128]{0,1:T(8,128)}, ...) | async-done | bytes 71565328 | tf_op jit(solution)/shard_map/psum | solution.py:91
  1592.1 21.0 %fusion.17 = f32[128,2048]{1,0:T(8,128)S(1)} fusion(f32[2,2048,2048]{2,1,0:T(8,128)} %param.20, f32[2048,128]{0,1:T(8,128)} %get-tuple-element.6), kind=kOutput, calls=%fused_computation.26 | convolution fusion | flops 6442713088 | bytes 18874368 | tf_op jit(solution)/shard_map/dot_general | solution.py:47
  1613.1 0.0 copy-start.1
  1613.1 0.0 copy-done
  1613.1 21.3 %fusion.19 = f32[128,2048]{1,0:T(8,128)S(1)} fusion(f32[2,2048,2048]{2,1,0:T(8,128)} %param.20, f32[2048,128]{0,1:T(8,128)S(1)} %copy-done), kind=kOutput, calls=%fused_computation.28 | convolution fusion | flops 6442713088 | bytes 18874368 | tf_op jit(solution)/shard_map/dot_general | solution.py:47
  1634.5 0.0 copy-done.5
  1634.5 1.8 convolution_bitcast_fusion.6
  1636.3 1.8 convolution_bitcast_fusion.5
  1638.1 0.0 copy-done.2
  1638.1 0.0 copy-done.6
  1638.1 1.8 fusion.55
  1640.0 0.0 copy-done.1
  1640.0 1.8 fusion.57
  1641.8 13.0 fusion.25
  1654.8 0.0 copy-start.7
  1654.8 0.0 copy-start.8
  1654.8 0.0 copy-start.9
  1654.9 0.0 copy-start.10
  1654.9 0.0 copy-start.11
  1654.9 0.0 copy-start.12
  1654.9 13.2 fusion.28
  1668.1 1.5 pad_maximum_fusion
  1669.6 1.5 pad_maximum_fusion.1
  1671.0 0.0 copy-done.7
  1671.0 0.0 copy-done.8
  1671.0 0.0 copy-done.9
  1671.0 0.0 copy-done.10
  1671.0 0.0 copy-done.11
  1671.0 0.0 copy-done.12
  1671.1 0.7 fusion.79
  1671.8 64.8 %fusion = (f32[2,2048,2048]{2,1,0:T(8,128)}, f32[2,2048,2048]{2,1,0:T(8,128)}) fusion(f32[1,2048,2048]{2,1,0:T(8,128)} %get-tuple-element.10, f32[1,2048,2048]{2,1,0:T(8,128)} %get-tuple-element.11, f32[2,2048,2048]{2,1,0:T(8,128)} %param.16, f32[1,2048,2048]{2,1,0:T(8,128)} %get-tuple-element.16, f32[1,2048,2048]{2,1,0:T(8,128)} %get-tuple-element.17, ...), kind=kLoop, calls=%fused_computation.8 | loop fusion | flops 67108864 | bytes 201326592 | tf_op jit(solution)/shard_map/add | solution.py:55
  (14 shorter events, 0.0 us)
Async XLA Ops:
  7.2 1585.0 %all-reduce.5.cloned.1.call-start = ((), (), s32[]{:S(2)}) async-start(), calls=%async_computation | async-start | bytes 143130624 | tf_op jit(solution)/shard_map/psum | solution.py:91
  24.1 373.1 %copy-start.3 = (bf16[2,2048,128]{2,1,0:T(8,128)(2,1)S(1)}, bf16[2,2048,128]{2,1,0:T(8,128)(2,1)}, u32[]{:S(2)}) copy-start(bf16[2,2048,128]{2,1,0:T(8,128)(2,1)} %param.14) | copy-start | bytes 3145732
  389.6 11.6 copy-start.4
  397.2 10.2 slice-start.2
  401.1 6.3 slice-start.3
  825.9 24.0 %slice-start = ((s8[8388608]{0:T(1024)(128)(4,1)}), s8[4194304]{0:T(1024)(128)(4,1)S(1)}, s32[]{:S(2)}) async-start(s8[8388608]{0:T(1024)(128)(4,1)} %bitcast.97), calls=%async_computation.1 | async-start | bytes 8388608
  828.4 21.5 %slice-start.1 = ((s8[8388608]{0:T(1024)(128)(4,1)}), s8[4194304]{0:T(1024)(128)(4,1)S(1)}, s32[]{:S(2)}) async-start(s8[8388608]{0:T(1024)(128)(4,1)} %bitcast.97), calls=%async_computation.2 | async-start | bytes 8388608
  828.4 42.5 %slice-start.4 = ((s8[8388608]{0:T(1024)(128)(4,1)}), s8[4194304]{0:T(1024)(128)(4,1)S(1)}, s32[]{:S(2)}) async-start(s8[8388608]{0:T(1024)(128)(4,1)} %bitcast.101), calls=%async_computation.5 | async-start | bytes 8388608
  849.8 21.1 %slice-start.5 = ((s8[8388608]{0:T(1024)(128)(4,1)}), s8[4194304]{0:T(1024)(128)(4,1)S(1)}, s32[]{:S(2)}) async-start(s8[8388608]{0:T(1024)(128)(4,1)} %bitcast.101), calls=%async_computation.6 | async-start | bytes 8388608
  1592.1 21.0 %copy-start = (f32[2048,128]{0,1:T(8,128)S(1)}, f32[2048,128]{0,1:T(8,128)}, u32[]{:S(2)}) copy-start(f32[2048,128]{0,1:T(8,128)} %get-tuple-element.7) | copy-start | bytes 3145732
  1592.1 42.3 %copy-start.5 = (f32[2,128,128]{2,1,0:T(8,128)S(1)}, f32[2,128,128]{2,1,0:T(8,128)}, u32[]{:S(2)}) copy-start(f32[2,128,128]{2,1,0:T(8,128)} %param.21) | copy-start | bytes 393220
  1592.1 46.0 %copy-start.2 = (f32[128,2048]{1,0:T(8,128)S(1)}, f32[128,2048]{1,0:T(8,128)}, u32[]{:S(2)}) copy-start(f32[128,2048]{1,0:T(8,128)} %get-tuple-element.8) | copy-start | bytes 3145732
  1592.1 46.0 %copy-start.6 = (f32[2,128,128]{2,1,0:T(8,128)S(1)}, f32[2,128,128]{2,1,0:T(8,128)}, u32[]{:S(2)}) copy-start(f32[2,128,128]{2,1,0:T(8,128)} %param.22) | copy-start | bytes 393220
  1613.1 26.8 %copy-start.1 = (f32[128,2048]{1,0:T(8,128)S(1)}, f32[128,2048]{1,0:T(8,128)}, u32[]{:S(2)}) copy-start(f32[128,2048]{1,0:T(8,128)} %get-tuple-element.9) | copy-start | bytes 3145732
  1654.8 16.2 copy-start.7
  1654.8 16.2 copy-start.8
  1654.8 16.2 copy-start.9
  1654.9 16.2 copy-start.10
  1654.9 16.2 copy-start.11
  1654.9 16.2 copy-start.12
Sparse Core Ops, SparseCore 0:
  892.2 699.8 all-reduce.4
where the time goes:
time: 1750 us; the launch traced here: 1740 us
  blocking collectives  725 us (41%)
  waiting for transfers between devices  700 us (40%)
  matrix products  214 us (12%)
  other arithmetic  90 us (5%)
    psum x1, waiting for transfers between devices, shard_body(): totals = lax.psum(local_sums, 'data')  700 us
    psum x1, blocking collectives, local_pass(): z_two = lax.psum(matmul(h_one, w_row[0]), 'model').astype(jnp.bfloat16)  365 us
    psum x1, blocking collectives, local_pass(): lax.psum(matmul_nt(g_three, w_col[1]), 'model').astype(jnp.bfloat16)  360 us
    dot_general x12, matrix products, matmul_tn(): lax.dot_general(left_mat, right_mat, TN_DIMS, preferred_element_type=jnp....  103 us
    dot_general x8, matrix products, exact_dot(): jnp.dot(left_mat, right_mat, precision=EXACT, preferred_element_type=jnp....  75.8 us
    add x2, other arithmetic, blend_factor(): FACTOR_DECAY * old_mats  65.6 us
  transfers between devices with their start and end apart: 1, of which 1 were waited for; matrix products, arithmetic and copies ran while one was open for 0% of the time, Pallas kernels for 0%

commit v1 on v0

v1 whole, which is shorter than its diff:
```python
import functools
import math
import jax
import jax.numpy as jnp
from jax import lax
from jax.experimental import pallas as pl
from jax.experimental.pallas import tpu as pltpu
from jax.sharding import PartitionSpec as P

FACTOR_DECAY = 0.8
GELU_SCALE = math.sqrt(2.0 / math.pi)
GELU_CUBIC = 0.044715
EXACT = lax.Precision.HIGHEST
TN_DIMS = (((0,), (0,)), ((), ()))
NT_DIMS = (((1,), (1,)), ((), ()))


def gelu_value(pre_act):
    tanh_arg = GELU_SCALE * (pre_act + GELU_CUBIC * pre_act * pre_act * pre_act)
    return 0.5 * pre_act * (1.0 + jnp.tanh(tanh_arg))


def gelu_slope(pre_act):
    tanh_arg = GELU_SCALE * (pre_act + GELU_CUBIC * pre_act * pre_act * pre_act)
    tanh_val = jnp.tanh(tanh_arg)
    return 0.5 * (1.0 + tanh_val) + 0.5 * pre_act * (1.0 - tanh_val * tanh_val) * GELU_SCALE * (1.0 + 3.0 * GELU_CUBIC * pre_act * pre_act)


def activate(pre_act):
    return gelu_value(pre_act.astype(jnp.float32)).astype(jnp.bfloat16)


def back_gate(grad_act, pre_act):
    return (grad_act.astype(jnp.float32) * gelu_slope(pre_act.astype(jnp.float32))).astype(jnp.bfloat16)


def matmul(left_mat, right_mat):
    return jnp.dot(left_mat, right_mat, preferred_element_type=jnp.float32)


def matmul_tn(left_mat, right_mat):
    return lax.dot_general(left_mat, right_mat, TN_DIMS, preferred_element_type=jnp.float32)


def matmul_nt(left_mat, right_mat):
    return lax.dot_general(left_mat, right_mat, NT_DIMS, preferred_element_type=jnp.float32)


def exact_dot(left_mat, right_mat):
    return jnp.dot(left_mat, right_mat, precision=EXACT, preferred_element_type=jnp.float32)


def precondition(a_inv, grad_mat, s_inv):
    return exact_dot(exact_dot(a_inv, grad_mat), s_inv)


def blend_factor(old_mats, first_new, second_new, inv_rows):
    return FACTOR_DECAY * old_mats + (1.0 - FACTOR_DECAY) * inv_rows * jnp.stack([first_new, second_new])


MESH = pl.DeviceIdType.MESH
SIDE = 4
PLANE = 16


def plane_peer(model_id, z_step, y_step):
    z_pos, y_pos = lax.rem(lax.div(model_id, SIDE) + z_step + SIDE, SIDE), lax.rem(lax.rem(model_id, SIDE) + y_step + SIDE, SIDE)
    return z_pos * SIDE + y_pos


class Copies:
    def __init__(self, send_sems, recv_sems):
        self.send_sems, self.recv_sems = send_sems, recv_sems
        self.index, self.sent = {}, []

    def slot(self, name):
        return self.index.setdefault(name, len(self.index))

    def make(self, name, src, dst, device):
        num = self.slot(name)
        return pltpu.make_async_remote_copy(src_ref=src, dst_ref=dst, send_sem=self.send_sems.at[num], recv_sem=self.recv_sems.at[num], device_id=device, device_id_type=MESH)

    def start(self, name, src, dst, device):
        copy = self.make(name, src, dst, device)
        copy.start()
        self.sent.append(copy)

    def wait(self, name, dst, device):
        self.make(name, dst, dst, device).wait_recv()

    def finish(self):
        for copy in self.sent:
            copy.wait_send()
        self.sent = []


def greet(devices):
    barrier = pltpu.get_barrier_semaphore()
    for device in devices:
        pl.semaphore_signal(barrier, inc=1, device_id=device, device_id_type=MESH)
    pl.semaphore_wait(barrier, len(devices))


def plane_gather(copies, tag, region, on_piece=None):
    model_id = lax.axis_index('model')

    def peer(order, first, second):
        return plane_peer(model_id, second, first) if order == 0 else plane_peer(model_id, first, second)

    def dev(order, first, second):
        return {'model': peer(order, first, second)}

    def send(order, name, owner, part, first, second):
        ref = region(owner, order, *part)
        copies.start((tag, order) + name, ref, ref, dev(order, first, second))

    def recv(order, name, owner, part):
        copies.wait((tag, order) + name, region(owner, order, *part), dev(order, 0, 1))

    whole, low, high = (0, 2), (0, 1), (1, 2)

    def spread(order, k):
        owner = peer(order, k, 0)
        send(order, ('b', k, -1), owner, whole, 0, 1)
        send(order, ('b', k, 1), owner, whole, 0, -1)

    def done(order, first, second):
        if on_piece is not None:
            on_piece(peer(order, first, second), order, (first, second))

    for order in (0, 1):
        owner = peer(order, 0, 0)
        send(order, ('a', -1), owner, whole, 1, 0)
        send(order, ('a', 1), owner, whole, -1, 0)
    for order in (0, 1):
        spread(order, 0)
    yield
    for order in (0, 1):
        for step, part in ((-1, low), (1, high)):
            owner = peer(order, step, 0)
            recv(order, ('a', step), owner, whole)
            send(order, ('a', 2 * step), owner, part, -step, 0)
            spread(order, step)
            done(order, step, 0)
        yield
    def pass_on(order, k):
        for step, part in ((-1, low), (1, high)):
            owner = peer(order, k, step)
            recv(order, ('b', k, step), owner, whole)
            send(order, ('b', k, 2 * step), owner, part, 0, -step)
            done(order, k, step)
    for order in (0, 1):
        pass_on(order, 0)
        yield
    for order in (0, 1):
        owner = peer(order, 2, 0)
        recv(order, ('a', -2), owner, low)
        recv(order, ('a', 2), owner, high)
        spread(order, 2)
        done(order, 2, 0)
        yield
    for k in (-1, 1, 2):
        for order in (0, 1):
            pass_on(order, k)
            yield
    for k in (0, -1, 1, 2):
        for order in (0, 1):
            owner = peer(order, k, 2)
            recv(order, ('b', k, -2), owner, low)
            recv(order, ('b', k, 2), owner, high)
            done(order, k, 2)
        yield


def neighbours():
    model_id = lax.axis_index('model')
    return [{'model': plane_peer(model_id, a, b)} for a, b in ((0, 1), (0, -1), (1, 0), (-1, 0))]


def partner():
    data_id = lax.axis_index('data')
    return {'data': data_id + 1 - 2 * lax.rem(data_id, 2)}


def gather_rows_kernel(rows, piece_ref, out_ref, local_sem, send_sems, recv_sems):
    model_id = lax.axis_index('model')
    copies = Copies(send_sems, recv_sems)
    out_ref[pl.ds(pl.multiple_of(model_id * rows, rows), rows), :] = piece_ref[...]
    greet(neighbours())

    def region(owner, order, lo, hi):
        start = owner * rows + order * (rows // 2) + lo * (rows // 4)
        return out_ref.at[pl.ds(pl.multiple_of(start, rows // 4), (hi - lo) * (rows // 4)), :]

    for _ in plane_gather(copies, 'g', region):
        pass
    copies.finish()


def gather_rows(piece, collective_id):
    rows, width = piece.shape
    return pl.pallas_call(
        functools.partial(gather_rows_kernel, rows),
        out_shape=jax.ShapeDtypeStruct((PLANE * rows, width), piece.dtype),
        in_specs=[pl.BlockSpec(memory_space=pltpu.VMEM)],
        out_specs=pl.BlockSpec(memory_space=pltpu.VMEM),
        scratch_shapes=[pltpu.SemaphoreType.DMA, pltpu.SemaphoreType.DMA((40,)), pltpu.SemaphoreType.DMA((40,))],
        compiler_params=pltpu.CompilerParams(collective_id=collective_id, has_side_effects=True),
    )(piece)


def gather_shared_kernel(rows, piece_ref, out_ref, send_sems, recv_sems):
    model_id = lax.axis_index('model')
    core = lax.rem(lax.axis_index('data'), 2)
    copies = Copies(send_sems, recv_sems)
    mate = partner()
    out_ref[pl.ds(pl.multiple_of(model_id * rows, rows), rows), :] = piece_ref[...]
    greet(neighbours() + [mate])
    half = rows // 2

    def region_of(which, owner, order, lo, hi):
        start = owner * rows + which * half + order * (half // 2) + lo * (half // 4)
        return out_ref.at[pl.ds(pl.multiple_of(start, half // 4), (hi - lo) * (half // 4)), :]

    handed = []
    def hand(owner, order, key):
        ref = region_of(core, owner, order, 0, 2)
        copies.start(('mate', order) + key, ref, ref, mate)
        handed.append((owner, order, key))

    for _ in plane_gather(copies, 'g', functools.partial(region_of, core), hand):
        pass
    for owner, order, key in handed:
        copies.wait(('mate', order) + key, region_of(1 - core, owner, order, 0, 2), mate)
    copies.finish()


def gather_shared(piece, collective_id):
    rows, width = piece.shape
    return pl.pallas_call(
        functools.partial(gather_shared_kernel, rows),
        out_shape=jax.ShapeDtypeStruct((PLANE * rows, width), piece.dtype),
        in_specs=[pl.BlockSpec(memory_space=pltpu.VMEM)],
        out_specs=pl.BlockSpec(memory_space=pltpu.VMEM),
        scratch_shapes=[pltpu.SemaphoreType.DMA((70,)), pltpu.SemaphoreType.DMA((70,))],
        compiler_params=pltpu.CompilerParams(collective_id=collective_id, has_side_effects=True),
    )(piece)


STEPS = [(a, b) for a in range(4) for b in range(4) if (a, b) != (0, 0)]


def swap_kernel(cols_ref, out_ref, send_sems, recv_sems):
    model_id = lax.axis_index('model')
    rows, width = out_ref.shape[0], cols_ref.shape[1]
    copies = Copies(send_sems, recv_sems)
    greet([{'model': plane_peer(model_id, a, b)} for a, b in STEPS])
    mine = pl.ds(pl.multiple_of(model_id * width, width), width)
    for a, b in STEPS:
        peer = plane_peer(model_id, a, b)
        copies.start((a, b), cols_ref.at[pl.ds(pl.multiple_of(peer * rows, rows), rows), :], out_ref.at[:, mine], {'model': peer})
    out_ref[:, mine] = cols_ref[pl.ds(pl.multiple_of(model_id * rows, rows), rows), :]
    for a, b in STEPS:
        peer = plane_peer(model_id, -a, -b)
        copies.wait((a, b), out_ref.at[:, pl.ds(pl.multiple_of(peer * width, width), width)], {'model': peer})
    copies.finish()


def swap(cols, collective_id):
    rows, width = cols.shape[0] // PLANE, cols.shape[1]
    return pl.pallas_call(
        swap_kernel,
        out_shape=jax.ShapeDtypeStruct((rows, PLANE * width), cols.dtype),
        in_specs=[pl.BlockSpec(memory_space=pltpu.VMEM)],
        out_specs=pl.BlockSpec(memory_space=pltpu.VMEM),
        scratch_shapes=[pltpu.SemaphoreType.DMA((15,)), pltpu.SemaphoreType.DMA((15,))],
        compiler_params=pltpu.CompilerParams(collective_id=collective_id, has_side_effects=True),
    )(cols)


def split_factor(left_cols, right_mat):
    return matmul_tn(left_cols, right_mat)


def solution(mesh):
    data_ways = mesh.shape['data']
    model_ways = mesh.shape['model']

    def shard_body(x_tokens, dy_tokens, w_col, w_row, a_old_col, s_old_col, a_old_row, s_old_row, a_inv_col, s_inv_col, a_inv_row, s_inv_row):
        model_id = lax.axis_index('model')
        data_id = lax.axis_index('data')
        width = x_tokens.shape[1]
        block = width // model_ways
        piece = block // data_ways
        inv_rows = 1.0 / (x_tokens.shape[0] * data_ways)

        def own_cols(mat):
            return lax.dynamic_slice_in_dim(mat, model_id * block, block, axis=1)

        def new_factor(local_rows, old_mat):
            total = lax.psum_scatter(local_rows, 'data', scatter_dimension=0, tiled=True)
            old_rows = lax.dynamic_slice_in_dim(old_mat, model_id * block + data_id * piece, piece, axis=0)
            mixed = FACTOR_DECAY * old_rows + (1.0 - FACTOR_DECAY) * inv_rows * total
            return lax.all_gather(mixed, ('model', 'data'), axis=0, tiled=True)

        z_one = matmul(x_tokens, w_col[0]).astype(jnp.bfloat16)
        h_one = activate(z_one)
        h_one_rows = swap(h_one, 0)
        w_two = gather_shared(w_row[0], 1)
        w_three_t = gather_shared(w_col[1].T, 2)
        z_two_rows = matmul(h_one_rows, w_two).astype(jnp.bfloat16)
        h_two = gather_rows(activate(z_two_rows), 3)
        z_three = matmul(h_two, w_col[1]).astype(jnp.bfloat16)
        h_three = activate(z_three)
        g_three = back_gate(matmul_nt(dy_tokens, w_row[1]).astype(jnp.bfloat16), z_three)
        dh_two_rows = matmul(swap(g_three, 4), w_three_t).astype(jnp.bfloat16)
        g_two = gather_rows(back_gate(dh_two_rows, z_two_rows), 5)
        g_one = back_gate(matmul_nt(g_two, w_row[0]).astype(jnp.bfloat16), z_one)

        a_new_col = jnp.stack([
            new_factor(split_factor(own_cols(x_tokens), x_tokens), a_old_col[0]),
            new_factor(split_factor(own_cols(h_two), h_two), a_old_col[1]),
        ])
        s_new_row = jnp.stack([
            new_factor(split_factor(own_cols(g_two), g_two), s_old_row[0]),
            new_factor(split_factor(own_cols(dy_tokens), dy_tokens), s_old_row[1]),
        ])
        small = lax.psum(jnp.stack([matmul_tn(mat, mat) for mat in (g_one, g_three, h_one, h_three)]), 'data')
        s_new_col = blend_factor(s_old_col, small[0], small[1], inv_rows)
        a_new_row = blend_factor(a_old_row, small[2], small[3], inv_rows)

        grads = [matmul_tn(x_tokens, g_one), matmul_tn(h_one, g_two), matmul_tn(h_two, g_three), matmul_tn(h_three, dy_tokens)]
        grads = [lax.psum(grad, 'data') * inv_rows for grad in grads]
        u_col = jnp.stack([precondition(a_inv_col[0], grads[0], s_inv_col[0]), precondition(a_inv_col[1], grads[2], s_inv_col[1])])
        u_row = jnp.stack([precondition(a_inv_row[0], grads[1], s_inv_row[0]), precondition(a_inv_row[1], grads[3], s_inv_row[1])])
        return (u_col, u_row, a_new_col, s_new_col, a_new_row, s_new_row)

    batch_split = P('data', None)
    col_split = P(None, None, 'model')
    row_split = P(None, 'model', None)
    replicated = P()
    return jax.shard_map(
        shard_body,
        mesh=mesh,
        in_specs=(batch_split, batch_split, col_split, row_split, replicated, row_split, row_split, replicated, replicated, row_split, row_split, replicated),
        out_specs=(col_split, row_split, replicated, row_split, row_split, replicated),
        check_vma=False,
    )
```

time: 1750 us -> 743 us (0.42)
  blocking collectives: 725 us -> 0 us
  waiting for transfers between devices: 700 us -> 266 us
  Pallas kernels: 0 us -> 203 us
  matrix products: 214 us -> 148 us
  local copies, waits for them, and re-layouts: 0.08 us -> 46.4 us
  other arithmetic: 90 us -> 57.6 us
    psum x2 -> x0, blocking collectives: 725 us -> none  [the longest x1 365 us: local_pass(): z_two = lax.psum(matmul(h_one, w_row[0]), 'model').astype(jnp.bfloat16)]
    psum x1, waiting for transfers between devices: 700 us -> 36.1 us  [shard_body(): grads = [lax.psum(grad, 'data') * inv_rows for grad in grads]]
    all_gather x0 -> x4, waiting for transfers between devices: none -> 229 us  [new_factor(): return lax.all_gather(mixed, ('model', 'data'), axis=0, tiled=True)]
    pallas_call x0 -> x6, Pallas kernels: none -> 203 us  [the longest x2 103 us: gather_rows(): pl.pallas_call(functools.partial(gather_rows_kernel, rows), out_shape=jax...]
    dot_general x12, matrix products: 103 us -> 34.8 us  [matmul_tn(): lax.dot_general(left_mat, right_mat, TN_DIMS, preferred_element_type=jnp....]
    add x2 -> x1, other arithmetic: 65.6 us -> 0.74 us  [blend_factor(): FACTOR_DECAY * old_mats]
    another operation x2 -> x5, other arithmetic: 2.92 us -> 50.3 us  [the longest x1 23.3 us: shard_body(): jnp.stack([new_factor(split_factor(own_cols(g_two), g_two), s_old_row[0])...]
    slice x0 -> x4, local copies, waits for them, and re-layouts: none -> 42.4 us  [the longest x1 21.2 us: shard_body(): a_old_col[0]]
  transfers between devices with their start and end apart: 1 -> 9, of which waited for: 1 -> 5; matrix products, arithmetic and copies ran while one was open for 0% -> 28% of each run, Pallas kernels for 0% -> 14%
where the time goes in v1:
time: 743 us; the launch traced here: 736 us
  waiting for transfers between devices  266 us (36%)
  Pallas kernels  203 us (27%)
  matrix products  148 us (20%)
  other arithmetic  57.6 us (8%)
  local copies, waits for them, and re-layouts  46.4 us (6%)
  between operations  14.7 us (2%)
    all_gather x4, waiting for transfers between devices, new_factor(): return lax.all_gather(mixed, ('model', 'data'), axis=0, tiled=True)  229 us
    pallas_call x2, Pallas kernels, gather_rows(): pl.pallas_call(functools.partial(gather_rows_kernel, rows), out_shape=jax...  103 us
    dot_general x8, matrix products, exact_dot(): jnp.dot(left_mat, right_mat, precision=EXACT, preferred_element_type=jnp....  75.4 us
    pallas_call x2, Pallas kernels, gather_shared(): pl.pallas_call(functools.partial(gather_shared_kernel, rows), out_shape=j...  70.3 us
    psum x1, waiting for transfers between devices, shard_body(): grads = [lax.psum(grad, 'data') * inv_rows for grad in grads]  36.1 us
    dot_general x12, matrix products, matmul_tn(): lax.dot_general(left_mat, right_mat, TN_DIMS, preferred_element_type=jnp....  34.8 us
    pallas_call x2, Pallas kernels, swap(): pl.pallas_call(swap_kernel, out_shape=jax.ShapeDtypeStruct((rows, PLANE *...  29 us
    dot_general x4, matrix products, matmul(): return jnp.dot(left_mat, right_mat, preferred_element_type=jnp.float32)  24.7 us
  transfers between devices with their start and end apart: 9, of which 5 were waited for; matrix products, arithmetic and copies ran while one was open for 28% of the time, Pallas kernels for 14%

profile of v1, /device:TPU:1, one launch (start us, length us, event | category | flops | bytes accessed | tf_op | source)
XLA Modules:
  0.0 736.2 jit_solution(9473723476514040639)
XLA Ops:
  7.2 0.0 reduce-scatter.7.cloned.1.call-start
  7.2 1.9 slice_bitcast_fusion.piece_ref
  9.1 6.8 fusion.41
  15.9 16.4 %shard_map.163 = bf16[128,2048]{1,0:T(8,128)(2,1)} custom-call(bf16[2048,128]{1,0:T(8,128)(2,1)} %get-tuple-element.17.cols_ref), custom_call_target="tpu_custom_call" | custom-call | tf_op jit(solution)/shard_map/pallas_call | solution.py:271
  32.3 35.0 %shard_map.164 = bf16[2048,2048]{1,0:T(8,128)(2,1)} custom-call(bf16[128,2048]{1,0:T(8,128)(2,1)} %slice_bitcast_fusion.piece_ref), custom_call_target="tpu_custom_call" | custom-call | tf_op jit(solution)/shard_map/pallas_call | solution.py:240
  67.4 5.9 fusion.37
  73.3 51.7 %shard_map.165 = bf16[2048,2048]{1,0:T(8,128)(2,1)} custom-call(bf16[128,2048]{1,0:T(8,128)(2,1)} %get-tuple-element.19.piece_ref), custom_call_target="tpu_custom_call" | custom-call | tf_op jit(solution)/shard_map/pallas_call | solution.py:202
  125.0 5.9 fusion.67
  130.8 0.0 reduce-scatter.7.cloned.1.call-update
  130.8 0.0 reduce-scatter.5.cloned.1.call-start
  130.9 5.9 fusion.69
  136.8 0.0 reduce-scatter.11.cloned.1.call-start
  136.8 5.9 fusion.63
  142.8 0.3 reduce-scatter.9.cloned.1.call-start
  143.0 5.9 convolution_convert_fusion.2
  148.9 1.0 copy.19
  150.0 6.9 fusion.24.cols_ref
  156.8 12.6 %shard_map.166 = bf16[128,2048]{1,0:T(8,128)(2,1)} custom-call(bf16[2048,128]{1,0:T(8,128)(2,1)} %fusion.24.cols_ref), custom_call_target="tpu_custom_call" | custom-call | tf_op jit(solution)/shard_map/pallas_call | solution.py:271
  169.4 35.3 %shard_map.167 = bf16[2048,2048]{1,0:T(8,128)(2,1)} custom-call(bf16[128,2048]{1,0:T(8,128)(2,1)} %bitcast.116), custom_call_target="tpu_custom_call" | custom-call | tf_op jit(solution)/shard_map/pallas_call | solution.py:240
  204.8 6.1 fusion.25.piece_ref
  210.9 51.7 %shard_map.168 = bf16[2048,2048]{1,0:T(8,128)(2,1)} custom-call(bf16[128,2048]{1,0:T(8,128)(2,1)} %fusion.25.piece_ref), custom_call_target="tpu_custom_call" | custom-call | tf_op jit(solution)/shard_map/pallas_call | solution.py:202
  262.6 5.9 fusion.65
  268.5 0.4 all-reduce.3.cloned.1.call-start
  269.0 0.3 convolution_bitcast_fusion.4
  269.4 0.9 convolution_bitcast_fusion.3
  270.3 0.3 convolution_bitcast_fusion.5
  270.6 6.3 fusion.26
  276.9 0.3 convolution_bitcast_fusion.6
  277.2 0.7 pad_maximum_fusion.4
  278.0 2.5 fusion.96
  280.5 2.3 convolution_bitcast_fusion
  282.8 2.3 fusion.102
  285.1 1.0 slice-done.7
  286.1 2.3 fusion.101
  288.4 0.0 all-gather.7.cloned.1.call-start
  288.5 21.2 %fusion.100 = (f32[1,2048,2048]{2,1,0:T(8,128)}, f32[1,2048,2048]{2,1,0:T(8,128)}) fusion(f32[2,2048,2048]{2,1,0:T(8,128)} %param.16), kind=kLoop, calls=%fused_computation.140 | loop fusion | bytes 67108864 | tf_op jit(solution)/shard_map/slice | solution.py:321
  309.7 1.6 bitcast_add_fusion.2
  311.4 0.0 all-gather.5.cloned.1.call-start
  311.4 0.0 reduce-scatter.5.cloned.1.call-done
  311.4 1.6 bitcast_add_fusion.3
  313.1 0.0 all-gather.11.cloned.1.call-start
  313.2 21.2 %fusion.99 = (f32[1,2048,2048]{2,1,0:T(8,128)}, f32[1,2048,2048]{2,1,0:T(8,128)}) fusion(f32[2,2048,2048]{2,1,0:T(8,128)} %param.19), kind=kLoop, calls=%fused_computation.139 | loop fusion | bytes 67108864 | tf_op jit(solution)/shard_map/slice | solution.py:325
  334.4 1.6 bitcast_add_fusion
  336.1 0.2 all-gather.9.cloned.1.call-start
  336.3 0.0 reduce-scatter.9.cloned.1.call-done
  336.3 1.6 bitcast_add_fusion.1
  338.0 36.1 %all-reduce.3.cloned.1.call-done = (f32[2048,128]{0,1:T(8,128)}, f32[2048,128]{0,1:T(8,128)}, f32[128,2048]{1,0:T(8,128)}, f32[128,2048]{1,0:T(8,128)}, f32[4,128,128]{2,1,0:T(8,128)}) async-done(((f32[2048,128]{0,1:T(8,128)}, f32[2048,128]{0,1:T(8,128)}, f32[128,2048]{1,0:T(8,128)}, f32[128,2048]{1,0:T(8,128)}, f32[4,128,128]{2,1,0:T(8,128)}), (f32[2048,128]{0,1:T(8,128)}, f32[2048,128]{0,1:T(8,128)}, ...) | async-done | bytes 4456464 | tf_op jit(solution)/shard_map/psum | solution.py:333
  374.1 20.9 %fusion.6 = f32[128,2048]{1,0:T(8,128)S(1)} fusion(f32[2,2048,2048]{2,1,0:T(8,128)} %param.20, f32[2048,128]{0,1:T(8,128)} %get-tuple-element.7), kind=kOutput, calls=%fused_computation.8 | convolution fusion | flops 6442713088 | bytes 18874368 | tf_op jit(solution)/shard_map/dot_general | solution.py:50
  395.0 1.8 convolution_bitcast_fusion.2
  396.9 21.0 %fusion.4 = f32[128,2048]{1,0:T(8,128)S(1)} fusion(f32[2,2048,2048]{2,1,0:T(8,128)} %param.20, f32[2048,128]{0,1:T(8,128)S(1)} %copy-done.3), kind=kOutput, calls=%fused_computation.6 | convolution fusion | flops 6442713088 | bytes 18874368 | tf_op jit(solution)/shard_map/dot_general | solution.py:50
  417.9 1.8 convolution_bitcast_fusion.1
  419.7 0.7 fusion.77
  420.5 1.5 pad_maximum_fusion.2
  421.9 1.8 fusion.54
  423.8 1.8 fusion.56
  425.6 13.0 %fusion.12 = f32[1,128,2048]{2,1,0:T(8,128)S(1)} fusion(f32[2048,128]{1,0:T(8,128)S(1)} %fusion.56, f32[2,2048,2048]{2,1,0:T(8,128)} %param.23), kind=kOutput, calls=%fused_computation.36 | convolution fusion | flops 6442450944 | bytes 18874368 | tf_op jit(solution)/shard_map/dot_general | solution.py:50
  438.6 13.3 %fusion.15 = f32[1,128,2048]{2,1,0:T(8,128)S(1)} fusion(f32[2048,128]{1,0:T(8,128)S(1)} %fusion.54, f32[2,2048,2048]{2,1,0:T(8,128)} %param.23), kind=kOutput, calls=%fused_computation.37 | convolution fusion | flops 6442450944 | bytes 18874368 | tf_op jit(solution)/shard_map/dot_general | solution.py:50
  451.9 1.5 pad_maximum_fusion.3
  453.4 5.7 all-gather.7.cloned.1.call-done
  459.1 82.3 %all-gather.5.cloned.1.call-done = f32[2048,2048]{1,0:T(8,128)} async-done(((f32[16,2048]{1,0:T(8,128)}), f32[2048,2048]{1,0:T(8,128)}) %all-gather.5.cloned.1.call-update) | async-done | bytes 16777232 | tf_op jit(solution)/shard_map/all_gather | solution.py:304
  541.3 23.3 %pad_maximum_fusion = f32[2,2048,2048]{2,1,0:T(8,128)} fusion(f32[1,2048,2048]{2,1,0:T(8,128)} %bitcast.112, f32[1,2048,2048]{2,1,0:T(8,128)} %bitcast.113), kind=kLoop, calls=%fused_computation | loop fusion | flops 8388608 | bytes 67108864 | tf_op jit(solution)/shard_map/stack | solution.py:320
  564.6 59.0 %all-gather.11.cloned.1.call-done = f32[2048,2048]{1,0:T(8,128)} async-done(((f32[16,2048]{1,0:T(8,128)}), f32[2048,2048]{1,0:T(8,128)}) %all-gather.11.cloned.1.call-update) | async-done | bytes 16777232 | tf_op jit(solution)/shard_map/all_gather | solution.py:304
  623.6 82.3 %all-gather.9.cloned.1.call-done = f32[2048,2048]{1,0:T(8,128)} async-done(((f32[16,2048]{1,0:T(8,128)}), f32[2048,2048]{1,0:T(8,128)}) %all-gather.9.cloned.1.call-update) | async-done | bytes 16777232 | tf_op jit(solution)/shard_map/all_gather | solution.py:304
  705.9 23.3 %pad_maximum_fusion.1 = f32[2,2048,2048]{2,1,0:T(8,128)} fusion(f32[1,2048,2048]{2,1,0:T(8,128)} %bitcast.114, f32[1,2048,2048]{2,1,0:T(8,128)} %bitcast.115), kind=kLoop, calls=%fused_computation.1 | loop fusion | flops 8388608 | bytes 67108864 | tf_op jit(solution)/shard_map/stack | solution.py:324
  (61 shorter events, 0.3 us)
Async XLA Ops:
  7.2 302.5 %reduce-scatter.7.cloned.1.call-start = ((), (), s32[]{:S(2)}) async-start(), calls=%async_computation.6 | async-start | bytes 1179648 | tf_op jit(solution)/shard_map/reduce_scatter | solution.py:301
  32.3 35.0 %copy-start.6 = (bf16[128,2048]{1,0:T(8,128)(2,1)S(1)}, bf16[128,2048]{1,0:T(8,128)(2,1)}, u32[]{:S(2)}) copy-start(bf16[128,2048]{1,0:T(8,128)(2,1)} %shard_map.163) | copy-start | bytes 1572868
  130.8 180.6 %reduce-scatter.5.cloned.1.call-start = ((), (), s32[]{:S(2)}) async-start(), calls=%async_computation.4 | async-start | bytes 1179648 | tf_op jit(solution)/shard_map/reduce_scatter | solution.py:301
  136.8 6.3 copy-start.2
  136.8 197.6 %reduce-scatter.11.cloned.1.call-start = ((), (), s32[]{:S(2)}) async-start(), calls=%async_computation.10 | async-start | bytes 1179648 | tf_op jit(solution)/shard_map/reduce_scatter | solution.py:301
  142.7 6.2 slice-start.8
  142.7 7.2 copy-start.9
  142.8 193.5 %reduce-scatter.9.cloned.1.call-start = ((), (), s32[]{:S(2)}) async-start(), calls=%async_computation.8 | async-start | bytes 1179648 | tf_op jit(solution)/shard_map/reduce_scatter | solution.py:301
  156.8 47.9 %copy-start.14 = (bf16[128,2048]{1,0:T(8,128)(2,1)S(1)}, bf16[128,2048]{1,0:T(8,128)(2,1)}, u32[]{:S(2)}) copy-start(bf16[128,2048]{1,0:T(8,128)(2,1)} %get-tuple-element.20) | copy-start | bytes 1572868
  169.4 35.3 %copy-start.7 = (bf16[128,2048]{1,0:T(8,128)(2,1)S(1)}, bf16[128,2048]{1,0:T(8,128)(2,1)}, u32[]{:S(2)}) copy-start(bf16[128,2048]{1,0:T(8,128)(2,1)} %shard_map.166) | copy-start | bytes 1572868
  262.6 6.4 copy-start
  262.6 7.7 %copy-start.1 = (bf16[2048,128]{1,0:T(8,128)(2,1)S(1)}, bf16[2048,128]{1,0:T(8,128)(2,1)}, u32[]{:S(2)}) copy-start(bf16[2048,128]{1,0:T(8,128)(2,1)} %fusion.24.cols_ref) | copy-start | bytes 1572868
  268.5 105.6 %all-reduce.3.cloned.1.call-start = ((), (), s32[]{:S(2)}) async-start(), calls=%async_computation.12 | async-start | bytes 8912896 | tf_op jit(solution)/shard_map/psum | solution.py:333
  269.3 8.7 %slice-start.2 = ((s8[8388608]{0:T(1024)(128)(4,1)}), s8[4194304]{0:T(1024)(128)(4,1)S(1)}, s32[]{:S(2)}) async-start(s8[8388608]{0:T(1024)(128)(4,1)} %bitcast.106), calls=%async_computation.15 | async-start | bytes 8388608
  270.6 9.9 %slice-start.4 = ((s8[8388608]{0:T(1024)(128)(4,1)}), s8[4194304]{0:T(1024)(128)(4,1)S(1)}, s32[]{:S(2)}) async-start(s8[8388608]{0:T(1024)(128)(4,1)} %bitcast.108), calls=%async_computation.17 | async-start | bytes 8388608
  270.6 7.4 %slice-start.3 = ((s8[8388608]{0:T(1024)(128)(4,1)}), s8[4194304]{0:T(1024)(128)(4,1)S(1)}, s32[]{:S(2)}) async-start(s8[8388608]{0:T(1024)(128)(4,1)} %bitcast.106), calls=%async_computation.16 | async-start | bytes 8388608
  270.6 9.9 %slice-start.5 = ((s8[8388608]{0:T(1024)(128)(4,1)}), s8[4194304]{0:T(1024)(128)(4,1)S(1)}, s32[]{:S(2)}) async-start(s8[8388608]{0:T(1024)(128)(4,1)} %bitcast.108), calls=%async_computation.18 | async-start | bytes 8388608
  278.0 4.8 slice-start
  280.5 2.3 slice-start.1
  280.5 4.6 slice-start.6
  282.8 3.3 slice-start.7
  288.4 170.6 %all-gather.7.cloned.1.call-start = ((), (), s32[]{:S(2)}) async-start(), calls=%async_computation.7 | async-start | bytes 16908288 | tf_op jit(solution)/shard_map/all_gather | solution.py:304
  311.4 230.0 %all-gather.5.cloned.1.call-start = ((), (), s32[]{:S(2)}) async-start(), calls=%async_computation.5 | async-start | bytes 16908288 | tf_op jit(solution)/shard_map/all_gather | solution.py:304
  313.1 310.5 %all-gather.11.cloned.1.call-start = ((), (), s32[]{:S(2)}) async-start(), calls=%async_computation.11 | async-start | bytes 16908288 | tf_op jit(solution)/shard_map/all_gather | solution.py:304
  336.1 369.8 %all-gather.9.cloned.1.call-start = ((), (), s32[]{:S(2)}) async-start(), calls=%async_computation.9 | async-start | bytes 16908288 | tf_op jit(solution)/shard_map/all_gather | solution.py:304
  374.1 20.9 %copy-start.10 = (f32[2,128,128]{2,1,0:T(8,128)S(1)}, f32[2,128,128]{2,1,0:T(8,128)}, u32[]{:S(2)}) copy-start(f32[2,128,128]{2,1,0:T(8,128)} %param.21) | copy-start | bytes 393220
  374.1 22.7 %copy-start.3 = (f32[2048,128]{0,1:T(8,128)S(1)}, f32[2048,128]{0,1:T(8,128)}, u32[]{:S(2)}) copy-start(f32[2048,128]{0,1:T(8,128)} %get-tuple-element.6) | copy-start | bytes 3145732
  396.9 22.9 %copy-start.8 = (f32[4,128,128]{2,1,0:T(8,128)S(1)}, f32[4,128,128]{2,1,0:T(8,128)}, u32[]{:S(2)}) copy-start(f32[4,128,128]{2,1,0:T(8,128)} %get-tuple-element.10) | copy-start | bytes 786436
  396.9 22.9 %copy-start.12 = (f32[2,128,128]{2,1,0:T(8,128)S(1)}, f32[2,128,128]{2,1,0:T(8,128)}, u32[]{:S(2)}) copy-start(f32[2,128,128]{2,1,0:T(8,128)} %param.18) | copy-start | bytes 393220
  396.9 22.9 %copy-start.13 = (f32[2,128,128]{2,1,0:T(8,128)S(1)}, f32[2,128,128]{2,1,0:T(8,128)}, u32[]{:S(2)}) copy-start(f32[2,128,128]{2,1,0:T(8,128)} %param.17) | copy-start | bytes 393220
  396.9 25.1 %copy-start.5 = (f32[128,2048]{1,0:T(8,128)S(1)}, f32[128,2048]{1,0:T(8,128)}, u32[]{:S(2)}) copy-start(f32[128,2048]{1,0:T(8,128)} %get-tuple-element.8) | copy-start | bytes 3145732
  396.9 25.0 %copy-start.11 = (f32[2,128,128]{2,1,0:T(8,128)S(1)}, f32[2,128,128]{2,1,0:T(8,128)}, u32[]{:S(2)}) copy-start(f32[2,128,128]{2,1,0:T(8,128)} %param.22) | copy-start | bytes 393220
  417.9 5.9 copy-start.4
Sparse Core Ops, SparseCore 0:
  131.0 29.3 reduce-scatter.6
  162.8 31.3 reduce-scatter.4
  196.6 31.1 reduce-scatter.10
  268.6 29.2 reduce-scatter.8
  301.0 73.0 all-reduce.2
  377.1 81.9 all-gather.6
  462.2 79.0 all-gather.4
  544.5 79.0 all-gather.10
  626.8 79.0 all-gather.8

commit v2 on v0

v2 whole, which is shorter than its diff:
```python
import contextlib
import functools
import math
import jax
import jax.numpy as jnp
from jax import lax
from jax.experimental import pallas as pl
from jax.experimental.pallas import tpu as pltpu
from jax.sharding import PartitionSpec as P

FACTOR_DECAY = 0.8
GELU_SCALE = math.sqrt(2.0 / math.pi)
GELU_CUBIC = 0.044715
EXACT = lax.Precision.HIGHEST
MESH = pl.DeviceIdType.MESH
SIDE = 4
PLANE = 16
DATA_WAYS = 8
WIDTH = 2048
BLOCK = 128
PIECE = 16
TRI = 9
ONLY = 0
CORES = 2
BOTH_WAYS = (1, -1)
ORDERS = (0, 1)
HALF = WIDTH // 2
SCOPED = False
FACTOR_COLS = TRI * BLOCK
GRAD_COLS = WIDTH + BLOCK
NT_DIMS = (((1,), (1,)), ((), ()))


def gelu_value(pre_act):
    tanh_arg = GELU_SCALE * (pre_act + GELU_CUBIC * pre_act * pre_act * pre_act)
    return 0.5 * pre_act * (1.0 + jnp.tanh(tanh_arg))


def gelu_slope(pre_act):
    tanh_arg = GELU_SCALE * (pre_act + GELU_CUBIC * pre_act * pre_act * pre_act)
    tanh_val = jnp.tanh(tanh_arg)
    return 0.5 * (1.0 + tanh_val) + 0.5 * pre_act * (1.0 - tanh_val * tanh_val) * GELU_SCALE * (1.0 + 3.0 * GELU_CUBIC * pre_act * pre_act)


def activate(pre_act):
    return gelu_value(pre_act.astype(jnp.float32)).astype(jnp.bfloat16)


def back_gate(grad_act, pre_act):
    return (grad_act.astype(jnp.float32) * gelu_slope(pre_act.astype(jnp.float32))).astype(jnp.bfloat16)


def matmul(left_mat, right_mat):
    return jnp.dot(left_mat, right_mat, preferred_element_type=jnp.float32)


def matmul_nt(left_mat, right_mat):
    return lax.dot_general(left_mat, right_mat, NT_DIMS, preferred_element_type=jnp.float32)


def exact_dot(left_mat, right_mat):
    return jnp.dot(left_mat, right_mat, precision=EXACT, preferred_element_type=jnp.float32)


def scope(name):
    return jax.named_scope(name) if SCOPED else contextlib.nullcontext()


def span_of(index, size):
    return pl.ds(pl.multiple_of(index * size, size), size)


class Place:
    def __init__(self):
        self.model, self.data = lax.axis_index('model'), lax.axis_index('data')
        self.core = lax.rem(self.data, 2)
        here = {'x': lax.div(self.data, 2), 'y': lax.rem(self.model, SIDE), 'z': lax.div(self.model, SIDE)}
        self.along = {dim: [at] + [lax.rem(at + step, SIDE) for step in range(1, SIDE)] for dim, at in here.items()}
        self.planes = [[z * SIDE + y for y in self.along['y']] for z in self.along['z']]
        self.lines = [x * 2 + self.core for x in self.along['x']]
        self.mate = (self.model, self.data + 1 - 2 * self.core)

    def at(self, dim, step):
        return self.along[dim][step % SIDE]

    def peer(self, z_step, y_step):
        return self.planes[z_step % SIDE][y_step % SIDE]

    def device(self, dim, step):
        if dim == 'x':
            return (self.model, self.lines[step % SIDE])
        return (self.peer(step, 0) if dim == 'z' else self.peer(0, step), self.data)


class Copies:
    def __init__(self, send_sems, recv_sems):
        self.send_sems, self.recv_sems = send_sems, recv_sems
        self.names, self.batches = {}, {}

    def start(self, batch, name, src, dst, device):
        num = self.names.setdefault((batch, name), len(self.names))
        out = self.batches.setdefault(batch, len(self.batches))
        pltpu.make_async_remote_copy(src_ref=src, dst_ref=dst, send_sem=self.send_sems.at[out], recv_sem=self.recv_sems.at[num], device_id=device, device_id_type=MESH).start()

    def wait(self, batch, name, ref):
        num = self.names.setdefault((batch, name), len(self.names))
        pltpu.make_async_copy(ref, ref, self.recv_sems.at[num]).wait()

    def left(self, batch, ref):
        pltpu.make_async_copy(ref, ref, self.send_sems.at[self.batches[batch]]).wait()


def call_out(devices):
    for device in devices:
        pl.semaphore_signal(pltpu.get_barrier_semaphore(), inc=1, device_id=device, device_id_type=MESH)


def all_here(devices):
    pl.semaphore_wait(pltpu.get_barrier_semaphore(), len(devices))


def plane_gather(copies, batch, place, region, like, on_piece):
    def steps(order, first, second):
        return (second, first) if order == 0 else (first, second)

    def send(order, name, k, part, first, second):
        z_step, y_step = steps(order, *k)
        ref = region(place.at('z', z_step), place.at('y', y_step), order, *part)
        copies.start(batch, name, ref, ref, (place.peer(*steps(order, first, second)), place.data))

    whole, low, high = (0, 2), (0, 1), (1, 2)

    def spread(order, k):
        for step in BOTH_WAYS:
            send(order, ('b', order, k), (k, 0), whole, 0, step)

    def pass_on(order, k):
        copies.wait(batch, ('b', order, k), like(4))
        for step, part in ((-1, low), (1, high)) if k != 2 else ((1, whole),):
            send(order, ('end', k), (k, step), part, 0, -step)
        for step in BOTH_WAYS:
            on_piece(order, *steps(order, k, step))

    for order in ORDERS:
        for step in BOTH_WAYS:
            send(order, 'a', (0, 0), whole, step, 0)
    for order in ORDERS:
        spread(order, 0)
    yield
    copies.wait(batch, 'a', like(8))
    for order in ORDERS:
        for step, part in ((-1, low), (1, high)):
            send(order, ('across', order), (step, 0), part, -step, 0)
            on_piece(order, *steps(order, step, 0))
    yield
    for step in BOTH_WAYS:
        for order in ORDERS:
            spread(order, step)
    yield
    for order in ORDERS:
        pass_on(order, 0)
        yield
    for order in ORDERS:
        copies.wait(batch, ('across', order), like(2))
        spread(order, 2)
        on_piece(order, *steps(order, 2, 0))
        yield
    for k in (-1, 1, 2):
        for order in ORDERS:
            pass_on(order, k)
            yield
    for k in (0, -1, 1, 2):
        copies.wait(batch, ('end', k), like(4))
        for order in ORDERS:
            on_piece(order, *steps(order, k, 2))
        yield


STEPS = [(a, b) for a in range(SIDE) for b in range(SIDE) if (a, b) != (0, 0)]


def line_reduce(copies, batch, place, src, near, far, store):
    core = place.core
    half = near.shape[1] // 2
    low, high = pl.ds(0, half), pl.ds(half, half)
    here, right, across, left = [place.at('x', step) for step in range(SIDE)]
    copies.start((batch, 'near'), ONLY, src.at[:, 1 - core], near, place.mate)
    yield
    copies.wait((batch, 'near'), ONLY, near)
    near[across] = near[across] + src[across, core]
    copies.start((batch, 'half'), 1, near.at[across, low], far.at[0, low], place.device('x', 1))
    copies.start((batch, 'half'), -1, near.at[across, high], far.at[0, high], place.device('x', -1))
    for there in (right, left, here):
        near[there] = near[there] + src[there, core]
    yield
    copies.wait((batch, 'half'), 1, far.at[0, low])
    near[right, low] = near[right, low] + far[0, low]
    copies.start((batch, 'full'), 1, near.at[right], far.at[1], place.device('x', 1))
    copies.wait((batch, 'half'), -1, far.at[0, high])
    near[left, high] = near[left, high] + far[0, high]
    copies.start((batch, 'full'), -1, near.at[left], far.at[2], place.device('x', -1))
    yield
    copies.wait((batch, 'full'), 1, far.at[1])
    copies.wait((batch, 'full'), -1, far.at[2])
    store(near[here] + far[1] + far[2])
    copies.left((batch, 'near'), near)
    copies.left((batch, 'half'), far.at[0])
    copies.left((batch, 'full'), far.at[pl.ds(1, 2)])
    yield


def line_gather(copies, batch, place, out):
    core = place.core
    half = out.shape[2] // 2
    here, right, across, left = [out.at[place.at('x', step), core] for step in range(SIDE)]

    def hand(ref):
        copies.start((batch, 'hand'), ONLY, ref, ref, place.mate)

    for step in BOTH_WAYS:
        copies.start((batch, 'all'), step, here, here, place.device('x', step))
    hand(here)
    yield
    for step, ref, span in ((1, left, pl.ds(0, half)), (-1, right, pl.ds(half, half))):
        copies.wait((batch, 'all'), step, ref)
        copies.start((batch, 'all'), 2 * step, ref.at[span], ref.at[span], place.device('x', step))
        hand(ref)
    yield
    for step, span in ((1, pl.ds(0, half)), (-1, pl.ds(half, half))):
        copies.wait((batch, 'all'), 2 * step, across.at[span])
    hand(across)
    yield
    copies.wait((batch, 'hand'), ONLY, out.at[:, 0])
    copies.left((batch, 'all'), out.at[0:3, 0])
    copies.left((batch, 'hand'), out.at[:, 0])
    yield


BALANCED = (('x', 'y', 'z'), ('y', 'z', 'x'), ('z', 'x', 'y'))
X_LAST = (('y', 'z', 'x'), ('z', 'y', 'x'))


def cube_gather(copies, batch, place, view, cuts, orders):
    core = place.core
    parts = [(order, pl.ds(start, end - start)) for order, start, end in zip(orders, cuts[:-1], cuts[1:])]
    every, low, high = (0, SIDE), (0, 2), (2, 2)

    def like(z, y, x):
        return view(0, *[pl.ds(0, num) if num > 1 else 0 for num in (z, y, x)], pl.ds(0, cuts[-1]))

    def at(order, cols, places):
        where = dict(zip(order, places))
        return view(core, where['z'], where['y'], where['x'], cols)

    def single(order, cols, step):
        return at(order, cols, (place.at(order[0], step), place.at(order[1], 0), place.at(order[2], 0)))

    def group(order, cols, a, b, span=every):
        return at(order, cols, (pl.ds(*span), place.at(order[1], a), place.at(order[2], b)))

    def hand(order, cols, a, b):
        ref = group(order, cols, a, b)
        copies.start((batch, 'mate'), ONLY, ref, ref, place.mate)

    def spread(order, cols, a):
        ref = group(order, cols, a, 0)
        for step in BOTH_WAYS:
            copies.start((batch, 'three'), a, ref, ref, place.device(order[2], step))
        hand(order, cols, a, 0)

    def pass_on(a):
        copies.wait((batch, 'three'), a, like(1, 2, SIDE))
        for order, cols in parts:
            for step, span in ((-1, low), (1, high)):
                half = group(order, cols, a, step, span)
                copies.start((batch, 'three'), ('end', a), half, half, place.device(order[2], -step))
                hand(order, cols, a, step)

    for order, cols in parts:
        for step in (2, 1, -1):
            copies.start((batch, 'one'), ONLY, single(order, cols, 0), single(order, cols, 0), place.device(order[0], step))
    yield
    copies.wait((batch, 'one'), ONLY, like(1, 1, 3))
    for order, cols in parts:
        for step in BOTH_WAYS:
            copies.start((batch, 'two'), ONLY, group(order, cols, 0, 0), group(order, cols, 0, 0), place.device(order[1], step))
    for order, cols in parts:
        spread(order, cols, 0)
    yield
    copies.wait((batch, 'two'), ONLY, like(1, 2, SIDE))
    for order, cols in parts:
        for step, span in ((-1, low), (1, high)):
            half = group(order, cols, step, 0, span)
            copies.start((batch, 'two'), 'end', half, half, place.device(order[1], -step))
    for order, cols in parts:
        for step in BOTH_WAYS:
            spread(order, cols, step)
    yield
    pass_on(0)
    yield
    copies.wait((batch, 'two'), 'end', like(1, 1, SIDE))
    for order, cols in parts:
        spread(order, cols, 2)
    yield
    for a in (-1, 1, 2):
        pass_on(a)
        yield
    for a in (0, -1, 1, 2):
        copies.wait((batch, 'three'), ('end', a), like(1, 1, SIDE))
        for order, cols in parts:
            hand(order, cols, a, 2)
        yield
    copies.wait((batch, 'mate'), ONLY, like(SIDE, SIDE, SIDE))
    copies.left((batch, 'mate'), like(SIDE, SIDE, SIDE))
    copies.left((batch, 'one'), like(1, 1, 3))
    copies.left((batch, 'two'), like(1, 3, SIDE))
    copies.left((batch, 'three'), like(3, SIDE, SIDE))
    yield


def pump(gen, name):
    with scope(name):
        next(gen, None)


def drain(gen, name):
    with scope(name):
        for _ in gen:
            pass


def step_kernel(scale, x_hbm, dy_hbm, w_col_hbm, w_row_hbm, a_old, s_old, a_inv, s_inv, fact, grads, w_col, w_row, x_buf, dy_buf, h_two, w_two, w_three, z_one, h_one, h_three,
                g_three, t_three, rows_buf, z_two, left, w_three_t, gram_src, gram_near, gram_far, old_buf, piece_buf, grad_src, grad_near,
                grad_far, grad_sum, grad_out, big_buf, load_sems, old_sems, big_sems, send_sems, recv_sems):
    place = Place()
    model_id, data_id, core = place.model, place.data, place.core
    spot, y_pos, z_pos = place.at('x', 0), place.at('y', 0), place.at('z', 0)
    copies = Copies(send_sems, recv_sems)
    my_rows = span_of(model_id, BLOCK)
    my_cols = span_of(model_id, BLOCK)
    my_part = pl.ds(pl.multiple_of(data_id * PIECE, PIECE), PIECE)
    g_one = t_three
    olds = [a_old.at[0], s_old.at[1], a_old.at[1], s_old.at[0]]
    chunk = 256
    n_chunks = WIDTH // chunk
    met = [(place.peer(a, b), data_id) for a, b in STEPS] + [place.mate] + [place.device('x', step) for step in (1, 2, 3)]

    def load(src, dst, base, i):
        rows = span_of(i, chunk)
        return pltpu.make_async_copy(src.at[rows, :], dst.at[rows, :], load_sems.at[base + i])

    def load_x(i):
        return load(x_hbm, x_buf, 0, i)

    def load_dy(i):
        return load(dy_hbm, dy_buf, n_chunks, i)

    def load_old(mat, j):
        rows = pl.ds(pl.multiple_of(model_id * BLOCK + data_id * PIECE, PIECE), PIECE)
        cols = span_of(lax.rem(model_id + j, PLANE), BLOCK)
        return pltpu.make_async_copy(olds[mat].at[rows, cols], old_buf.at[mat, :, pl.ds(j * BLOCK, BLOCK)], old_sems.at[mat])

    def cols_of(buf, cols):
        return buf[:, cols] if len(buf.shape) == 2 else buf[:, :, :, :, :, cols].reshape(WIDTH, cols.size)

    def rows_of(buf, z_step, y_step):
        return buf[place.at('z', z_step), place.at('y', y_step)].reshape(BLOCK, WIDTH)

    call_out(met)
    own_w_two = pltpu.make_async_copy(w_row_hbm.at[0, my_part, :], w_two.at[z_pos, y_pos, spot, core], old_sems.at[4])
    own_w_two.start()
    load_w = [pltpu.make_async_copy(w_col_hbm, w_col, big_sems.at[0]), pltpu.make_async_copy(w_row_hbm, w_row, big_sems.at[1])]
    for move in load_w:
        move.start()
    for i in range(n_chunks):
        load_x(i).start()

    def z_one_step(i, carry):
        rows = span_of(i, chunk)
        load_x(i).wait()
        pre_act = matmul(x_buf[rows, :], w_col[0]).astype(jnp.bfloat16)
        z_one[rows, :] = pre_act
        h_one[rows, :] = activate(pre_act)
        return carry

    own_w_two.wait()
    with scope('greet'):
        all_here(met)

    def z_one_first():
        with scope('z1a'):
            for move in load_w:
                move.wait()
            w_three_t[...] = w_col[1].T
            w_three[z_pos, y_pos, spot, core] = w_three_t[my_part, :]
            lax.fori_loop(0, n_chunks // 2, z_one_step, 0)
        for i in range(n_chunks):
            load_dy(i).start()
        for mat in range(4):
            for j in range(TRI):
                load_old(mat, j).start()

    def weight_thread(batch, buf, cuts, orders):
        def view(which, z, y, x, cols):
            return buf.at[z, y, x, which, :, cols]
        return cube_gather(copies, batch, place, view, cuts, orders)

    def z_one_rest():
        with scope('z1b'):
            lax.fori_loop(n_chunks // 2, n_chunks, z_one_step, 0)

    def send_block(batch, cols_ref, a, b):
        peer = place.peer(a, b)
        copies.start(batch, ONLY, cols_ref.at[span_of(peer, BLOCK), :], rows_buf.at[:, my_cols], (peer, data_id))

    def wait_blocks(batch):
        others = rows_buf.at[:, 0:WIDTH - BLOCK]
        copies.wait(batch, ONLY, others)
        copies.left(batch, others)

    loaded = []

    def wait_dy():
        if not loaded:
            for i in range(n_chunks):
                load_dy(i).wait()
            loaded.append(True)

    def t_three_step(i, carry):
        rows = span_of(i, chunk)
        t_three[rows, :] = matmul_nt(dy_buf[rows, :], w_row[1]).astype(jnp.bfloat16)
        return carry

    def t_three_part(num):
        wait_dy()
        with scope('t3'):
            lax.fori_loop(num * n_chunks // 4, (num + 1) * n_chunks // 4, t_three_step, 0)

    def turn(dst, src, cols):
        for i in range(4):
            rows = slice(i * 512, (i + 1) * 512)
            dst[:, rows] = (src[rows, cols] if len(src.shape) == 2 else src[i, :, :, :, :, cols].reshape(512, BLOCK)).T

    def gram_product(mat, lhs, right):
        def block_cols(j):
            return cols_of(right, span_of(lax.rem(model_id + j, PLANE), BLOCK))

        def gram_step(i, carry):
            block = matmul(lhs[...], jnp.concatenate([block_cols(2 * i), block_cols(2 * i + 1)], axis=1))
            gram_src[mat, :, :, :, span_of(i, chunk)] = block.reshape(SIDE, CORES, PIECE, chunk)
            return carry
        lax.fori_loop(0, TRI // 2, gram_step, 0)
        block = matmul(lhs[...], block_cols(TRI - 1))
        gram_src[mat, :, :, :, (TRI - 1) * BLOCK:] = block.reshape(SIDE, CORES, PIECE, BLOCK)

    def grad_product(lhs, right, same, slot):
        def grad_step(i, carry):
            cols = span_of(i, chunk)
            block = matmul(lhs[...], cols_of(right, cols))
            grad_src[slot, :, :, :, cols] = block.reshape(SIDE, CORES, PIECE, chunk)
            return carry
        lax.fori_loop(0, n_chunks, grad_step, 0)
        block = matmul(lhs[...], same[...])
        grad_src[slot, :, :, :, WIDTH:GRAD_COLS] = block.reshape(SIDE, CORES, PIECE, BLOCK)

    def store_factor(mat, total):
        pltpu.make_async_copy(old_buf.at[mat], old_buf.at[mat], old_sems.at[mat]).wait()
        mixed = FACTOR_DECAY * old_buf[mat] + scale * total
        piece_buf[mat] = mixed

    def sum_thread(mat):
        return line_reduce(copies, ('gram', mat), place, gram_src.at[mat], gram_near.at[mat], gram_far.at[mat], functools.partial(store_factor, mat))

    def factor_thread(first, count, cuts, orders):
        mats = pl.ds(first, count)

        def view(which, z, y, x, cols):
            return fact.at[z, y, x, which, mats, :, cols]

        move = pltpu.make_async_copy(piece_buf.at[mats], fact.at[z_pos, y_pos, spot, core, mats], old_sems.at[4])
        move.start()
        move.wait()
        yield from cube_gather(copies, ('fact', first), place, view, cuts, orders)

    def gram_job(mat, slot, right):
        if mat == 1:
            wait_dy()
        with scope('gram'):
            turn(left.at[slot], right, my_cols)
            gram_product(mat, left.at[slot], right)

    def grad_job(layer, slot, lhs, right):
        with scope('dW'):
            turn(left.at[slot], lhs, slice(0, BLOCK))
            grad_product(left.at[slot], right, lhs, layer % 2)
        if layer == 0:
            load_big(0, 0).start()
            load_big(0, 1).start()

    def swap_first():
        for a, b in STEPS:
            send_block('h1', h_one, a, b)
        rows_buf[:, my_cols] = h_one[my_rows, :]

    def z_two_step(i, carry):
        cols = span_of(i, chunk)
        pre_act = matmul(rows_buf[...], cols_of(w_two, cols)).astype(jnp.bfloat16)
        z_two[:, cols] = pre_act
        h_two[z_pos, y_pos, :, :, :, cols] = activate(pre_act).reshape(SIDE, CORES, PIECE, chunk)
        return carry

    def second_forward():
        drain(threads['w2'], 'w2_rest')
        with scope('wait_h1'):
            wait_blocks('h1')
        with scope('z2'):
            lax.fori_loop(0, n_chunks, z_two_step, 0)

    def forward_block(a, b):
        rows = span_of(place.peer(a, b), BLOCK)
        pre_act = matmul(rows_of(h_two, a, b), w_col[1]).astype(jnp.bfloat16)
        h_three[rows, :] = activate(pre_act)
        g_three[rows, :] = back_gate(t_three[rows, :], pre_act)
        if (a, b) != (0, 0):
            send_block('g3', g_three, a, b)

    def backward_block(a, b):
        rows = span_of(place.peer(a, b), BLOCK)
        grad = matmul_nt(rows_of(w_two, a, b), w_row[0]).astype(jnp.bfloat16)
        g_one[rows, :] = back_gate(grad, z_one[rows, :])

    def gather_tokens(tag, buf, block_step):
        seen = {}

        def on_piece(order, first, second):
            where = (first % SIDE, second % SIDE)
            seen[where] = seen.get(where, 0) + 1

        def region(z, y, order, lo, hi):
            return buf.at[z, y, pl.ds(2 * order + lo, hi - lo)]

        def like(quarters):
            return x_buf.at[0:quarters * BLOCK // 4, :]

        done = {(0, 0)}
        gen = plane_gather(copies, tag, place, region, like, on_piece)
        next(gen)
        with scope(tag + '_blocks'):
            block_step(0, 0)
        yield
        for _ in gen:
            ready = [where for where in sorted(seen) if seen[where] == 2 and where not in done]
            with scope(tag + '_blocks'):
                for where in ready:
                    block_step(*where)
            done.update(ready)
            yield
        copies.left(tag, x_buf.at[0:WIDTH - BLOCK, :])

    def split(value):
        high = value.astype(jnp.bfloat16)
        rest = value - high.astype(jnp.float32)
        middle = rest.astype(jnp.bfloat16)
        return high, middle, (rest - middle.astype(jnp.float32)).astype(jnp.bfloat16)

    inverses = [s_inv.at[1], a_inv.at[1], s_inv.at[0], a_inv.at[0]]
    big_rows = 2 * PIECE

    def load_big(layer, i):
        slot = lax.rem(i, 2)
        return pltpu.make_async_copy(inverses[layer].at[span_of(i, chunk), span_of(core, HALF)], big_buf.at[slot], big_sems.at[slot])

    def grad_thread(layer):
        sum_ref, out_ref, tag = grad_sum.at[layer], grad_out.at[layer], ('grad', layer)

        def keep_sum(total):
            sum_ref[core] = total

        def big_step(i, carry):
            load_big(layer, i).wait()
            lhs = jnp.concatenate(split(sum_ref[:, :, span_of(i, chunk)].reshape(big_rows, chunk)), axis=0)
            high, middle, low = split(big_buf[lax.rem(i, 2)])
            by_high, by_middle, by_low = matmul(lhs, high), matmul(lhs[:2 * big_rows], middle), matmul(lhs[:big_rows], low)
            small = by_high[2 * big_rows:] + by_middle[big_rows:] + by_low
            out_ref[:, :HALF] += by_high[:big_rows] + (by_high[big_rows:2 * big_rows] + by_middle[:big_rows] + small)

            @pl.when(i + 2 < n_chunks)
            def _():
                load_big(layer, i + 2).start()
            if layer < 3:
                @pl.when(i + 2 >= n_chunks)
                def _():
                    load_big(layer + 1, i + 2 - n_chunks).start()
            return carry

        yield from line_reduce(copies, tag, place, grad_src.at[layer % 2], grad_near.at[layer], grad_far.at[layer], keep_sum)
        copies.start(tag + ('pair',), ONLY, sum_ref.at[core], sum_ref.at[core], place.mate)
        yield
        copies.wait(tag + ('pair',), ONLY, sum_ref.at[1 - core])
        copies.left(tag + ('pair',), sum_ref.at[0])
        out_ref[...] = jnp.concatenate([jnp.zeros((big_rows, HALF), jnp.float32), sum_ref[:, :, WIDTH:].reshape(big_rows, BLOCK)], axis=1)
        with scope('X'):
            lax.fori_loop(0, n_chunks // 2, big_step, 0)
        yield
        with scope('X'):
            lax.fori_loop(n_chunks // 2, n_chunks, big_step, 0)
        move = pltpu.make_async_copy(out_ref, grads.at[layer, spot, core], old_sems.at[5])
        move.start()
        move.wait()
        yield from line_gather(copies, tag, place, grads.at[layer])

    def g_two_step(i, carry):
        cols = span_of(i, chunk)
        grad = matmul(rows_buf[...], cols_of(w_three, cols)).astype(jnp.bfloat16)
        w_two[z_pos, y_pos, :, :, :, cols] = back_gate(grad, z_two[:, cols]).reshape(SIDE, CORES, PIECE, chunk)
        return carry

    def second_backward():
        drain(threads['w3'], 'w3_rest')
        with scope('wait_g3'):
            wait_blocks('g3')
            rows_buf[:, my_cols] = g_three[my_rows, :]
        with scope('g2'):
            lax.fori_loop(0, n_chunks, g_two_step, 0)

    threads = dict(
        w2=weight_thread('w2', w_two, W_TWO_CUTS, BALANCED),
        w3=weight_thread('w3', w_three, W_THREE_CUTS, MOSTLY_X),
        h2=gather_tokens('h2', h_two, forward_block),
        g2=gather_tokens('g2', w_two, backward_block),
        pair=factor_thread(0, 2, PAIR_CUTS, MOSTLY_X),
        fa3=factor_thread(2, 1, LATE_CUTS, BALANCED),
        fs2=factor_thread(3, 1, LATE_CUTS, BALANCED),
        sum0=sum_thread(0), sum1=sum_thread(1), sum2=sum_thread(2), sum3=sum_thread(3),
        grad4=grad_thread(0), grad3=grad_thread(1), grad2=grad_thread(2), grad1=grad_thread(3),
    )
    steps = {name: functools.partial(pump, thread, name) for name, thread in threads.items()}
    steps.update(
        z0=z_one_first, z1=z_one_rest, swap=swap_first, z2=second_forward, back=second_backward,
        A1=functools.partial(gram_job, 0, 0, x_buf), S4=functools.partial(gram_job, 1, 1, dy_buf),
        A3=functools.partial(gram_job, 2, 0, h_two), S2=functools.partial(gram_job, 3, 0, w_two),
        dW4=functools.partial(grad_job, 0, 1, h_three, dy_buf), dW3=functools.partial(grad_job, 1, 0, g_three, h_two),
        dW2=functools.partial(grad_job, 2, 0, h_one, w_two), dW1=functools.partial(grad_job, 3, 1, g_one, x_buf),
        t0=functools.partial(t_three_part, 0), t1=functools.partial(t_three_part, 1),
        t2=functools.partial(t_three_part, 2), t3=functools.partial(t_three_part, 3),
    )
    for step in plan(**steps):
        step()
    for name, thread in threads.items():
        drain(thread, name)
    assert len(copies.batches) == N_BATCHES and len(copies.names) == N_COPIES, (len(copies.batches), len(copies.names))


W_TWO_CUTS = (0, 384, 1536, 2048)
W_THREE_CUTS = (0, 1152, 1920, 2048)
PAIR_CUTS = (0, 384, 1024, 1152)
LATE_CUTS = (0, 512, 640, 1152)
MOSTLY_X = (('y', 'z', 'x'), ('z', 'y', 'x'), ('x', 'y', 'z'))


def plan(w2, w3, h2, g2, pair, fa3, fs2, sum0, sum1, sum2, sum3, grad4, grad3, grad2, grad1, z0, z1, swap, z2, back, A1, S4, A3, S2, dW4, dW3, dW2, dW1, t0, t1, t2, t3):
    return (
        w2, z0, w2, t3, w3, t2, w2, z1, w2, A1, w2, t0, swap, S4, sum1, sum0, w2, sum0, w2, w2, w2, t1, sum1, w3, w2, w2, sum0, w2, sum1, w3, w2, z2,
        h2, sum0, sum1, w3, pair, h2, h2, w3, pair, h2, w3, h2, h2, h2, h2, w3, w3, h2, h2, w3, h2, pair, h2, w3, w3, h2, w3, h2, h2, h2, w3, h2,
        pair, pair, A3, sum2, dW3, pair, back, g2, g2, dW4, grad3, grad4, g2, g2, sum2, grad3, g2, g2, grad4, pair, sum2, g2, grad4, grad3, g2, sum2,
        g2, grad4, fa3, grad4, g2, grad4, grad3, g2, g2, pair, grad3, grad4, g2, g2, grad3, g2, pair, fa3, g2, pair, grad3, g2, S2, fa3, sum3, dW2,
        sum3, grad4, grad2, fa3, sum3, pair, grad2, fa3, dW1, sum3, fa3, grad1, fs2, grad2, grad1, fs2, grad2, grad2, grad1, grad3, pair, grad2, fa3,
        fs2, fa3, fs2, grad1, grad1, pair, grad2, grad1, fs2, grad1, grad4, fa3, fa3, grad3, fs2, fa3, fs2, grad4, grad2, fs2, grad1, fs2, fs2, fa3,
        fs2, grad2, grad3, fs2, grad1, fs2, grad2, fa3, grad1,
    )


N_BATCHES = 60
N_COPIES = 156


def step_call(x_tokens, dy_tokens, w_col, w_row, a_old, s_old, a_inv, s_inv, scale):
    f32, bf16 = jnp.float32, jnp.bfloat16
    tall, wide = (WIDTH, BLOCK), (BLOCK, WIDTH)
    cube = (SIDE, SIDE, SIDE, 2)
    rows = 2 * PIECE
    hbm = pl.BlockSpec(memory_space=pl.ANY)
    scratch = [pltpu.VMEM((2,) + tall, bf16), pltpu.VMEM((2,) + wide, bf16)] + [pltpu.VMEM((WIDTH, WIDTH), bf16)] * 2 + [pltpu.VMEM(cube + (PIECE, WIDTH), bf16)] * 3
    scratch += [pltpu.VMEM(tall, bf16)] * 5 + [pltpu.VMEM(wide, bf16)] * 2 + [pltpu.VMEM((2,) + wide, bf16), pltpu.VMEM(wide, bf16)]
    scratch += [pltpu.VMEM((4, SIDE, CORES, PIECE, TRI * BLOCK), f32), pltpu.VMEM((4, SIDE, PIECE, TRI * BLOCK), f32), pltpu.VMEM((4, 3, PIECE, TRI * BLOCK), f32)]
    scratch += [pltpu.VMEM((4, PIECE, TRI * BLOCK), f32), pltpu.VMEM((4, PIECE, FACTOR_COLS), f32)]
    scratch += [pltpu.VMEM((2, SIDE, CORES, PIECE, GRAD_COLS), f32), pltpu.VMEM((4, SIDE, PIECE, GRAD_COLS), f32), pltpu.VMEM((4, 3, PIECE, GRAD_COLS), f32)]
    scratch += [pltpu.VMEM((4, 2, PIECE, GRAD_COLS), f32), pltpu.VMEM((4, rows, HALF + BLOCK), f32), pltpu.VMEM((2, 256, HALF), f32)]
    scratch += [pltpu.SemaphoreType.DMA((num,)) for num in (16, 6, 2, N_BATCHES, N_COPIES)]
    return pl.pallas_call(
        functools.partial(step_kernel, scale),
        out_shape=[jax.ShapeDtypeStruct(cube + (4, PIECE, FACTOR_COLS), f32), jax.ShapeDtypeStruct((4, SIDE, 2, rows, HALF + BLOCK), f32)],
        in_specs=[hbm] * 8,
        out_specs=[hbm, hbm],
        scratch_shapes=scratch,
        compiler_params=pltpu.CompilerParams(collective_id=0, has_side_effects=True, vmem_limit_bytes=67043328),
        name='step',
    )(x_tokens, dy_tokens, w_col, w_row, a_old, s_old, a_inv, s_inv)


def finish_kernel(scale, inv_rows, fact, grads, s_old_col, a_old_row, s_inv_col, a_inv_row, a_new, s_new, u_col, u_row, s_new_col, a_new_row, buf, turned, sums, u_col_buf, u_row_buf, load_sems, out_sems, turn_sems, small_sems):
    outs = [(a_new, 0), (s_new, 1), (a_new, 1), (s_new, 0)]

    def load(mat, row):
        z, y = lax.div(row, SIDE), lax.rem(row, SIDE)
        return pltpu.make_async_copy(fact.at[z, y, :, :, mat], buf.at[mat, row], load_sems.at[mat * PLANE + row])

    def turn_done(slot):
        return pltpu.make_async_copy(turned.at[slot], turned.at[slot], turn_sems.at[slot])

    def start_load(mat):
        def body(row, carry):
            load(mat, row).start()
            return carry
        lax.fori_loop(0, PLANE, body, 0)

    load_sums = pltpu.make_async_copy(grads, sums, out_sems.at[4])
    load_sums.start()
    for mat in range(4):
        start_load(mat)
    half = HALF

    def new_blocks():
        load_sums.wait()
        for layer in range(4):
            block, num = scale * sums[layer, :, 0, :, half:].reshape(BLOCK, BLOCK), 1 - layer // 2
            if layer % 2 == 1:
                s_new_col[num] = FACTOR_DECAY * s_old_col[num] + block
            else:
                a_new_row[num] = FACTOR_DECAY * a_old_row[num] + block

    def move_small(batch):
        moves = [(u_col_buf, u_col), (u_row_buf, u_row)]
        return [pltpu.make_async_copy(src.at[1 - batch], dst.at[1 - batch], small_sems.at[2 * batch + num]) for num, (src, dst) in enumerate(moves)]

    chunk = 2 * BLOCK

    def small_product(layer, i):
        num = 1 - layer // 2
        core, cols, out = lax.div(i, SIDE), span_of(lax.rem(i, SIDE), chunk), span_of(i, chunk)
        product = sums[layer, :, core, :, cols].reshape(BLOCK, chunk)
        if layer % 2 == 1:
            u_col_buf[num, out, :] = exact_dot(product.T, s_inv_col[num]) * inv_rows
        else:
            u_row_buf[num, :, out] = exact_dot(a_inv_row[num], product) * inv_rows

    for mat, (out, num) in enumerate(outs):
        def row_step(row, carry):
            load(mat, row).wait()
            slot = lax.rem(row, 2)
            if mat in (1, 2):
                @pl.when(row < PLANE // 2)
                def _():
                    small_product(2 * mat - 2, row)

                @pl.when(row >= PLANE // 2)
                def _():
                    small_product(2 * mat - 1, row - PLANE // 2)
            for j in range(TRI):
                cols = span_of(lax.rem(row + j, PLANE), BLOCK)
                pltpu.make_async_copy(buf.at[mat, row, :, :, :, pl.ds(j * BLOCK, BLOCK)], out.at[num, row, :, :, :, cols], out_sems.at[mat]).start()
            if mat > 0:
                turn_done(slot).wait()
            else:
                @pl.when(row >= 2)
                def _():
                    turn_done(slot).wait()
            for j in range(1, TRI - 1):
                other = lax.rem(row + j, PLANE)
                block = buf[mat, row, :, :, :, j * BLOCK:(j + 1) * BLOCK].reshape(BLOCK, BLOCK).T
                turned[slot, j - 1] = block.reshape(SIDE, CORES, PIECE, BLOCK)
                pltpu.make_async_copy(turned.at[slot, j - 1], out.at[num, other, :, :, :, span_of(row, BLOCK)], turn_sems.at[slot]).start()
            return carry

        if mat == 1:
            new_blocks()
        lax.fori_loop(0, PLANE, row_step, 0)
        if mat in (1, 2):
            for move in move_small(mat - 1):
                move.start()
    for batch in range(2):
        for move in move_small(batch):
            move.wait()
    for slot in range(2):
        turn_done(slot).wait()
    for mat in range(4):
        pltpu.make_async_copy(buf.at[mat], buf.at[mat], out_sems.at[mat]).wait()


def finish_call(fact, grads, s_old_col, a_old_row, s_inv_col, a_inv_row, scale, inv_rows):
    f32 = jnp.float32
    shapes = [(2, PLANE, SIDE, CORES, PIECE, WIDTH)] * 2 + [(2, WIDTH, BLOCK), (2, BLOCK, WIDTH)] + [(2, BLOCK, BLOCK)] * 2
    hbm, vmem = pl.BlockSpec(memory_space=pl.ANY), pl.BlockSpec(memory_space=pltpu.VMEM)
    return pl.pallas_call(
        functools.partial(finish_kernel, scale, inv_rows),
        out_shape=[jax.ShapeDtypeStruct(shape, f32) for shape in shapes],
        in_specs=[hbm] * 2 + [vmem] * 4,
        out_specs=[hbm] * 4 + [vmem] * 2,
        scratch_shapes=[pltpu.VMEM((4, PLANE, SIDE, CORES, PIECE, FACTOR_COLS), f32), pltpu.VMEM((2, TRI - 2, SIDE, CORES, PIECE, BLOCK), f32), pltpu.VMEM(grads.shape, f32), pltpu.VMEM((2, WIDTH, BLOCK), f32), pltpu.VMEM((2, BLOCK, WIDTH), f32)] + [pltpu.SemaphoreType.DMA((num,)) for num in (4 * PLANE, 5, 2, 4)],
        compiler_params=pltpu.CompilerParams(vmem_limit_bytes=67043328),
        name='finish',
    )(fact, grads, s_old_col, a_old_row, s_inv_col, a_inv_row)


def solution(mesh):
    def shard_body(x_tokens, dy_tokens, w_col, w_row, a_old_col, s_old_col, a_old_row, s_old_row, a_inv_col, s_inv_col, a_inv_row, s_inv_row):
        inv_rows = 1.0 / (x_tokens.shape[0] * DATA_WAYS)
        scale = (1.0 - FACTOR_DECAY) * inv_rows
        fact, grads = step_call(x_tokens, dy_tokens, w_col, w_row, a_old_col, s_old_row, a_inv_col, s_inv_row, scale)
        a_new_col, s_new_row, u_col, u_row, s_new_col, a_new_row = finish_call(fact, grads, s_old_col, a_old_row, s_inv_col, a_inv_row, scale, inv_rows)
        return (u_col, u_row, a_new_col.reshape(2, WIDTH, WIDTH), s_new_col, a_new_row, s_new_row.reshape(2, WIDTH, WIDTH))

    batch_split = P('data', None)
    col_split = P(None, None, 'model')
    row_split = P(None, 'model', None)
    replicated = P()
    return jax.shard_map(
        shard_body,
        mesh=mesh,
        in_specs=(batch_split, batch_split, col_split, row_split, replicated, row_split, row_split, replicated, replicated, row_split, row_split, replicated),
        out_specs=(col_split, row_split, replicated, row_split, row_split, replicated),
        check_vma=False,
    )
```

time: 1750 us -> 258 us (0.15)
  blocking collectives: 725 us -> 0 us
  waiting for transfers between devices: 700 us -> 0 us
  Pallas kernels: 0 us -> 257 us
  matrix products: 214 us -> 0 us
  other arithmetic: 90 us -> 0 us
    psum x2 -> x0, blocking collectives: 725 us -> none  [the longest x1 365 us: local_pass(): z_two = lax.psum(matmul(h_one, w_row[0]), 'model').astype(jnp.bfloat16)]
    psum x1 -> x0, waiting for transfers between devices: 700 us -> none  [shard_body(): totals = lax.psum(local_sums, 'data')]
    pallas_call x0 -> x2, Pallas kernels: none -> 257 us  [the longest x1 218 us: step_call(): pl.pallas_call(functools.partial(step_kernel, scale), out_shape=[jax.Shap...]
    dot_general x26 -> x0, matrix products: 214 us -> none  [the longest x12 103 us: matmul_tn(): lax.dot_general(left_mat, right_mat, TN_DIMS, preferred_element_type=jnp....]
    add x2 -> x0, other arithmetic: 65.6 us -> none  [blend_factor(): FACTOR_DECAY * old_mats]
    convert_element_type x2 -> x0, other arithmetic: 21.5 us -> none  [the longest x1 13.9 us: back_gate(): (grad_act.astype(jnp.float32) * gelu_slope(pre_act.astype(jnp.float32)))....]
  transfers between devices with their start and end apart: 1 -> 0, of which waited for: 1 -> 0; matrix products, arithmetic and copies ran while one was open for 0% -> 0% of each run, Pallas kernels for 0% -> 0%
where the time goes in v2:
time: 258 us
  Pallas kernels  257 us (100%)
    pallas_call x1, Pallas kernels, step_call(): pl.pallas_call(functools.partial(step_kernel, scale), out_shape=[jax.Shap...  218 us
    pallas_call x1, Pallas kernels, finish_call(): pl.pallas_call(functools.partial(finish_kernel, scale, inv_rows), out_sha...  38.6 us

profile of v2, /device:TPU:1, one launch (start us, length us, event | category | flops | bytes accessed | tf_op | source)
XLA Modules:
  0.0 257.9 jit_solution(927593573502419977)
XLA Ops:
  0.6 218.5 %step.1 = (f32[4,4,4,2,4,16,1152]{6,5,4,3,2,1,0:T(8,128)}, f32[4,4,2,32,1152]{4,3,2,1,0:T(8,128)}) custom-call(bf16[2048,2048]{1,0:T(8,128)(2,1)} %x_hbm.1, bf16[2048,2048]{1,0:T(8,128)(2,1)} %dy_hbm.1, bf16[2,2048,128]{2,1,0:T(8,128)(2,1)} %w_col_hbm.1, bf16[2,128,2048]{2,1,0:T(8,128)(2,1)} %w_row_hbm.1, f32[2,2048,2048]{2,1,0:T(8,128)} %a_old.1, ...), custom_call_target="tpu_custom_call" | custom-call | tf_op jit(solution)/shard_map/step/pallas_call | solution.py:690
  219.1 38.6 %finish.1 = (f32[2,16,4,2,16,2048]{5,4,3,2,1,0:T(8,128)}, f32[2,16,4,2,16,2048]{5,4,3,2,1,0:T(8,128)}, f32[2,2048,128]{2,1,0:T(8,128)}, f32[2,128,2048]{2,1,0:T(...) custom-call(f32[4,4,4,2,4,16,1152]{6,5,4,3,2,1,0:T(8,128)} %get-tuple-element.14.fact, ...), custom_call_target="tpu_custom_call" | custom-call | tf_op jit(solution)/shard_map/finish/pallas_call | solution.py:794

commit v3 on v2

--- a/solution.py
+++ b/solution.py
@@ -240,20 +240,20 @@
 X_LAST = (('y', 'z', 'x'), ('z', 'y', 'x'))
 
 
-def cube_gather(copies, batch, place, view, cuts, orders):
+def cube_gather(copies, batch, place, view, cuts, orders, one_way, owners=SIDE):
     core = place.core
     parts = [(order, pl.ds(start, end - start)) for order, start, end in zip(orders, cuts[:-1], cuts[1:])]
-    every, low, high = (0, SIDE), (0, 2), (2, 2)
+    every, low, high = (0, owners), (0, owners // 2), (owners // 2, owners // 2)
 
     def like(z, y, x):
-        return view(0, *[pl.ds(0, num) if num > 1 else 0 for num in (z, y, x)], pl.ds(0, cuts[-1]))
+        return view(0, *[pl.ds(0, num) if num > 1 else 0 for num in (z, y, x)], pl.ds(cuts[0], cuts[-1] - cuts[0]))
 
     def at(order, cols, places):
         where = dict(zip(order, places))
         return view(core, where['z'], where['y'], where['x'], cols)
 
-    def single(order, cols, step):
-        return at(order, cols, (place.at(order[0], step), place.at(order[1], 0), place.at(order[2], 0)))
+    def single(order, cols):
+        return at(order, cols, [place.at(dim, 0) for dim in order])
 
     def group(order, cols, a, b, span=every):
         return at(order, cols, (pl.ds(*span), place.at(order[1], a), place.at(order[2], b)))
@@ -268,28 +268,41 @@
             copies.start((batch, 'three'), a, ref, ref, place.device(order[2], step))
         hand(order, cols, a, 0)
 
+    def ways(single_way, dim):
+        return ((1, every),) if single_way and dim != 'x' else ((-1, low), (1, high))
+
     def pass_on(a):
-        copies.wait((batch, 'three'), a, like(1, 2, SIDE))
+        copies.wait((batch, 'three'), a, like(1, CORES, owners))
         for order, cols in parts:
-            for step, span in ((-1, low), (1, high)):
+            for step, span in ways(a in one_way, order[2]):
                 half = group(order, cols, a, step, span)
                 copies.start((batch, 'three'), ('end', a), half, half, place.device(order[2], -step))
+            for step in BOTH_WAYS:
                 hand(order, cols, a, step)
 
-    for order, cols in parts:
-        for step in (2, 1, -1):
-            copies.start((batch, 'one'), ONLY, single(order, cols, 0), single(order, cols, 0), place.device(order[0], step))
-    yield
-    copies.wait((batch, 'one'), ONLY, like(1, 1, 3))
+    def first_sends():
+        for order, cols in parts:
+            for step in (2, 1, -1):
+                copies.start((batch, 'one'), ONLY, single(order, cols), single(order, cols), place.device(order[0], step))
+
+    if owners == SIDE:
+        first_sends()
+        yield
+        copies.wait((batch, 'one'), ONLY, like(1, 1, 3))
+    else:
+        pl.when(place.at('z', 0) < owners)(first_sends)
+        yield
+        pl.when(place.at('z', 0) < owners)(lambda: copies.wait((batch, 'one'), ONLY, like(1, 1, 1)))
+        pl.when(place.at('z', 0) >= owners)(lambda: copies.wait((batch, 'one'), ONLY, like(1, 1, owners)))
     for order, cols in parts:
         for step in BOTH_WAYS:
             copies.start((batch, 'two'), ONLY, group(order, cols, 0, 0), group(order, cols, 0, 0), place.device(order[1], step))
     for order, cols in parts:
         spread(order, cols, 0)
     yield
-    copies.wait((batch, 'two'), ONLY, like(1, 2, SIDE))
+    copies.wait((batch, 'two'), ONLY, like(1, CORES, owners))
     for order, cols in parts:
-        for step, span in ((-1, low), (1, high)):
+        for step, span in ways(len(one_way) > 2, order[1]):
             half = group(order, cols, step, 0, span)
             copies.start((batch, 'two'), 'end', half, half, place.device(order[1], -step))
     for order, cols in parts:
@@ -298,7 +311,7 @@
     yield
     pass_on(0)
     yield
-    copies.wait((batch, 'two'), 'end', like(1, 1, SIDE))
+    copies.wait((batch, 'two'), 'end', like(1, 1, owners))
     for order, cols in parts:
         spread(order, cols, 2)
     yield
@@ -306,15 +319,19 @@
         pass_on(a)
         yield
     for a in (0, -1, 1, 2):
-        copies.wait((batch, 'three'), ('end', a), like(1, 1, SIDE))
+        copies.wait((batch, 'three'), ('end', a), like(1, 1, owners))
         for order, cols in parts:
             hand(order, cols, a, 2)
         yield
-    copies.wait((batch, 'mate'), ONLY, like(SIDE, SIDE, SIDE))
-    copies.left((batch, 'mate'), like(SIDE, SIDE, SIDE))
-    copies.left((batch, 'one'), like(1, 1, 3))
-    copies.left((batch, 'two'), like(1, 3, SIDE))
-    copies.left((batch, 'three'), like(3, SIDE, SIDE))
+    whole = like(SIDE, SIDE, owners)
+    copies.wait((batch, 'mate'), ONLY, whole)
+    copies.left((batch, 'mate'), whole)
+    if owners == SIDE:
+        copies.left((batch, 'one'), like(1, 1, 3))
+    else:
+        pl.when(place.at('z', 0) < owners)(lambda: copies.left((batch, 'one'), like(1, 1, 3)))
+    copies.left((batch, 'two'), like(1, 3, owners))
+    copies.left((batch, 'three'), like(3, SIDE, owners))
     yield
 
 
@@ -343,6 +360,7 @@
     olds = [a_old.at[0], s_old.at[1], a_old.at[1], s_old.at[0]]
     chunk = 256
     n_chunks = WIDTH // chunk
+    half_way = n_chunks // CORES
     met = [(place.peer(a, b), data_id) for a, b in STEPS] + [place.mate] + [place.device('x', step) for step in (1, 2, 3)]
 
     def load(src, dst, base, i):
@@ -393,21 +411,21 @@
                 move.wait()
             w_three_t[...] = w_col[1].T
             w_three[z_pos, y_pos, spot, core] = w_three_t[my_part, :]
-            lax.fori_loop(0, n_chunks // 2, z_one_step, 0)
+            lax.fori_loop(0, half_way, z_one_step, 0)
         for i in range(n_chunks):
             load_dy(i).start()
         for mat in range(4):
             for j in range(TRI):
                 load_old(mat, j).start()
 
-    def weight_thread(batch, buf, cuts, orders):
+    def weight_thread(batch, buf, cuts, orders, one_way):
         def view(which, z, y, x, cols):
             return buf.at[z, y, x, which, :, cols]
-        return cube_gather(copies, batch, place, view, cuts, orders)
+        return cube_gather(copies, batch, place, view, cuts, orders, one_way)
 
     def z_one_rest():
         with scope('z1b'):
-            lax.fori_loop(n_chunks // 2, n_chunks, z_one_step, 0)
+            lax.fori_loop(half_way, n_chunks, z_one_step, 0)
 
     def send_block(batch, cols_ref, a, b):
         peer = place.peer(a, b)
@@ -431,10 +449,12 @@
         t_three[rows, :] = matmul_nt(dy_buf[rows, :], w_row[1]).astype(jnp.bfloat16)
         return carry
 
-    def t_three_part(num):
+    def t_three_thread():
         wait_dy()
-        with scope('t3'):
-            lax.fori_loop(num * n_chunks // 4, (num + 1) * n_chunks // 4, t_three_step, 0)
+        for i in range(0, n_chunks, CORES):
+            with scope('t3'):
+                lax.fori_loop(i, i + CORES, t_three_step, 0)
+            yield
 
     def turn(dst, src, cols):
         for i in range(4):
@@ -471,7 +491,7 @@
     def sum_thread(mat):
         return line_reduce(copies, ('gram', mat), place, gram_src.at[mat], gram_near.at[mat], gram_far.at[mat], functools.partial(store_factor, mat))
 
-    def factor_thread(first, count, cuts, orders):
+    def factor_thread(first, count, cuts, orders, one_way, rest_order):
         mats = pl.ds(first, count)
 
         def view(which, z, y, x, cols):
@@ -480,7 +500,12 @@
         move = pltpu.make_async_copy(piece_buf.at[mats], fact.at[z_pos, y_pos, spot, core, mats], old_sems.at[4])
         move.start()
         move.wait()
-        yield from cube_gather(copies, ('fact', first), place, view, cuts, orders)
+        main = cube_gather(copies, ('fact', first), place, view, cuts, orders, one_way)
+        rest = cube_gather(copies, ('rest', first), place, view, (TRI * BLOCK - BLOCK, FACTOR_COLS), (rest_order,), (), CORES)
+        for _ in main:
+            next(rest)
+            yield
+
 
     def gram_job(mat, slot, right):
         if mat == 1:
@@ -496,6 +521,50 @@
         if layer == 0:
             load_big(0, 0).start()
             load_big(0, 1).start()
+
+    near_by = [(a, b) for a in range(SIDE) for b in range(SIDE) if 2 not in (a, b)]
+    far_off = [where for where in [(0, 0)] + STEPS if where not in near_by]
+
+    def picked(buf, places, cols):
+        if len(buf.shape) == 2:
+            parts = [buf[span_of(place.peer(a, b), BLOCK), cols] for a, b in places]
+        else:
+            parts = [buf[place.at('z', a), place.at('y', b), :, :, :, cols] for a, b in places]
+        return [part.reshape(BLOCK, part.shape[-1]) for part in parts]
+
+    def turn_picked(slot, buf, places, cols):
+        for num, part in enumerate(picked(buf, places, cols)):
+            left[slot, :, num * BLOCK:(num + 1) * BLOCK] = part.T
+
+    def put(dst, cols, product, places):
+        value = product.reshape(SIDE, CORES, PIECE, product.shape[-1])
+        dst[:, :, :, cols] = value if places is near_by else dst[:, :, :, cols] + value
+
+    def late_grad(layer, slot, lhs, right, places):
+        def late_step(i, carry):
+            cols = span_of(i, chunk)
+            put(dst, cols, matmul(left[slot, :, :depth], jnp.concatenate(picked(right, places, cols), axis=0)), places)
+            return carry
+
+        dst, depth, block = grad_src.at[layer % 2], len(places) * BLOCK, slice(0, BLOCK)
+        with scope('dW'):
+            turn_picked(slot, lhs, places, block)
+            lax.fori_loop(0, n_chunks, late_step, 0)
+            put(dst, slice(WIDTH, GRAD_COLS), matmul(left[slot, :, :depth], jnp.concatenate(picked(lhs, places, block), axis=0)), places)
+
+    def late_gram(mat, slot, right, places):
+        def block_cols(j):
+            return jnp.concatenate(picked(right, places, span_of(lax.rem(model_id + j, PLANE), BLOCK)), axis=0)
+
+        def late_step(i, carry):
+            put(dst, span_of(i, chunk), matmul(left[slot, :, :depth], jnp.concatenate([block_cols(2 * i), block_cols(2 * i + 1)], axis=1)), places)
+            return carry
+
+        dst, depth = gram_src.at[mat], len(places) * BLOCK
+        with scope('gram'):
+            turn_picked(slot, right, places, my_cols)
+            lax.fori_loop(0, TRI // 2, late_step, 0)
+            put(dst, slice((TRI - 1) * BLOCK, FACTOR_COLS), matmul(left[slot, :, :depth], block_cols(TRI - 1)), places)
 
     def swap_first():
         for a, b in STEPS:
@@ -567,7 +636,7 @@
     big_rows = 2 * PIECE
 
     def load_big(layer, i):
-        slot = lax.rem(i, 2)
+        slot = lax.rem(i, CORES)
         return pltpu.make_async_copy(inverses[layer].at[span_of(i, chunk), span_of(core, HALF)], big_buf.at[slot], big_sems.at[slot])
 
     def grad_thread(layer):
@@ -579,7 +648,7 @@
         def big_step(i, carry):
             load_big(layer, i).wait()
             lhs = jnp.concatenate(split(sum_ref[:, :, span_of(i, chunk)].reshape(big_rows, chunk)), axis=0)
-            high, middle, low = split(big_buf[lax.rem(i, 2)])
+            high, middle, low = split(big_buf[lax.rem(i, CORES)])
             by_high, by_middle, by_low = matmul(lhs, high), matmul(lhs[:2 * big_rows], middle), matmul(lhs[:big_rows], low)
             small = by_high[2 * big_rows:] + by_middle[big_rows:] + by_low
             out_ref[:, :HALF] += by_high[:big_rows] + (by_high[big_rows:2 * big_rows] + by_middle[:big_rows] + small)
@@ -600,10 +669,10 @@
         copies.left(tag + ('pair',), sum_ref.at[0])
         out_ref[...] = jnp.concatenate([jnp.zeros((big_rows, HALF), jnp.float32), sum_ref[:, :, WIDTH:].reshape(big_rows, BLOCK)], axis=1)
         with scope('X'):
-            lax.fori_loop(0, n_chunks // 2, big_step, 0)
+            lax.fori_loop(0, half_way, big_step, 0)
         yield
         with scope('X'):
-            lax.fori_loop(n_chunks // 2, n_chunks, big_step, 0)
+            lax.fori_loop(half_way, n_chunks, big_step, 0)
         move = pltpu.make_async_copy(out_ref, grads.at[layer, spot, core], old_sems.at[5])
         move.start()
         move.wait()
@@ -624,25 +693,26 @@
             lax.fori_loop(0, n_chunks, g_two_step, 0)
 
     threads = dict(
-        w2=weight_thread('w2', w_two, W_TWO_CUTS, BALANCED),
-        w3=weight_thread('w3', w_three, W_THREE_CUTS, MOSTLY_X),
+        w2=weight_thread('w2', w_two, W_TWO_CUTS, BALANCED, W_TWO_WAYS),
+        w3=weight_thread('w3', w_three, W_THREE_CUTS, MOSTLY_X, W_THREE_WAYS),
         h2=gather_tokens('h2', h_two, forward_block),
         g2=gather_tokens('g2', w_two, backward_block),
-        pair=factor_thread(0, 2, PAIR_CUTS, MOSTLY_X),
-        fa3=factor_thread(2, 1, LATE_CUTS, BALANCED),
-        fs2=factor_thread(3, 1, LATE_CUTS, BALANCED),
+        pair=factor_thread(0, 2, PAIR_CUTS, MOSTLY_X, PAIR_WAYS, ('z', 'y', 'x')),
+        fa3=factor_thread(2, 1, LATE_CUTS, BALANCED, LATE_WAYS, ('z', 'x', 'y')),
+        fs2=factor_thread(3, 1, LATE_CUTS, BALANCED, LATE_WAYS, ('z', 'x', 'y')),
         sum0=sum_thread(0), sum1=sum_thread(1), sum2=sum_thread(2), sum3=sum_thread(3),
+        t3=t_three_thread(),
         grad4=grad_thread(0), grad3=grad_thread(1), grad2=grad_thread(2), grad1=grad_thread(3),
     )
     steps = {name: functools.partial(pump, thread, name) for name, thread in threads.items()}
     steps.update(
         z0=z_one_first, z1=z_one_rest, swap=swap_first, z2=second_forward, back=second_backward,
         A1=functools.partial(gram_job, 0, 0, x_buf), S4=functools.partial(gram_job, 1, 1, dy_buf),
-        A3=functools.partial(gram_job, 2, 0, h_two), S2=functools.partial(gram_job, 3, 0, w_two),
+        A3=functools.partial(gram_job, 2, 0, h_two),
+        S2a=functools.partial(late_gram, 3, 0, w_two, near_by), S2b=functools.partial(late_gram, 3, 0, w_two, far_off),
         dW4=functools.partial(grad_job, 0, 1, h_three, dy_buf), dW3=functools.partial(grad_job, 1, 0, g_three, h_two),
-        dW2=functools.partial(grad_job, 2, 0, h_one, w_two), dW1=functools.partial(grad_job, 3, 1, g_one, x_buf),
-        t0=functools.partial(t_three_part, 0), t1=functools.partial(t_three_part, 1),
-        t2=functools.partial(t_three_part, 2), t3=functools.partial(t_three_part, 3),
+        dW2a=functools.partial(late_grad, 2, 0, h_one, w_two, near_by), dW2b=functools.partial(late_grad, 2, 0, h_one, w_two, far_off),
+        dW1a=functools.partial(late_grad, 3, 1, g_one, x_buf, near_by), dW1b=functools.partial(late_grad, 3, 1, g_one, x_buf, far_off),
     )
     for step in plan(**steps):
         step()
@@ -651,27 +721,31 @@
     assert len(copies.batches) == N_BATCHES and len(copies.names) == N_COPIES, (len(copies.batches), len(copies.names))
 
 
-W_TWO_CUTS = (0, 384, 1536, 2048)
-W_THREE_CUTS = (0, 1152, 1920, 2048)
-PAIR_CUTS = (0, 384, 1024, 1152)
-LATE_CUTS = (0, 512, 640, 1152)
+W_TWO_CUTS = (0, 640, 1408, 2048)
+W_THREE_CUTS = (0, 896, 1920, 2048)
+PAIR_CUTS = (0, 384, 896, 1024)
+LATE_CUTS = (0, 512, 640, 1024)
+W_TWO_WAYS = (-1, 1, 2)
+W_THREE_WAYS = (-1, 0)
+PAIR_WAYS = (0, 1)
+LATE_WAYS = ()
 MOSTLY_X = (('y', 'z', 'x'), ('z', 'y', 'x'), ('x', 'y', 'z'))
 
 
-def plan(w2, w3, h2, g2, pair, fa3, fs2, sum0, sum1, sum2, sum3, grad4, grad3, grad2, grad1, z0, z1, swap, z2, back, A1, S4, A3, S2, dW4, dW3, dW2, dW1, t0, t1, t2, t3):
+def plan(w2, w3, h2, g2, pair, fa3, fs2, sum0, sum1, sum2, sum3, grad4, grad3, grad2, grad1, z0, z1, swap, z2, back, A1, S4, A3, S2a, S2b, dW4, dW3, dW2a, dW2b, dW1a, dW1b, t3):
     return (
-        w2, z0, w2, t3, w3, t2, w2, z1, w2, A1, w2, t0, swap, S4, sum1, sum0, w2, sum0, w2, w2, w2, t1, sum1, w3, w2, w2, sum0, w2, sum1, w3, w2, z2,
-        h2, sum0, sum1, w3, pair, h2, h2, w3, pair, h2, w3, h2, h2, h2, h2, w3, w3, h2, h2, w3, h2, pair, h2, w3, w3, h2, w3, h2, h2, h2, w3, h2,
-        pair, pair, A3, sum2, dW3, pair, back, g2, g2, dW4, grad3, grad4, g2, g2, sum2, grad3, g2, g2, grad4, pair, sum2, g2, grad4, grad3, g2, sum2,
-        g2, grad4, fa3, grad4, g2, grad4, grad3, g2, g2, pair, grad3, grad4, g2, g2, grad3, g2, pair, fa3, g2, pair, grad3, g2, S2, fa3, sum3, dW2,
-        sum3, grad4, grad2, fa3, sum3, pair, grad2, fa3, dW1, sum3, fa3, grad1, fs2, grad2, grad1, fs2, grad2, grad2, grad1, grad3, pair, grad2, fa3,
-        fs2, fa3, fs2, grad1, grad1, pair, grad2, grad1, fs2, grad1, grad4, fa3, fa3, grad3, fs2, fa3, fs2, grad4, grad2, fs2, grad1, fs2, fs2, fa3,
-        fs2, grad2, grad3, fs2, grad1, fs2, grad2, fa3, grad1,
+        w2, w2, z0, w3, w2, z1, w2, A1, sum0, w2, S4, sum1, swap, sum0, sum1, w2, t3, t3, t3, w2, sum0, sum1, w2, w3, t3, w2, sum0, w2, w2, sum1, w2,
+        pair, w2, w3, z2, h2, pair, h2, w3, h2, w3, h2, pair, h2, h2, h2, h2, w3, h2, h2, h2, h2, h2, h2, pair, w3, h2, w3, h2, w3, w3, pair, h2, w3,
+        w3, pair, pair, A3, w3, back, g2, dW3, sum2, g2, dW4, grad4, grad3, grad4, g2, sum2, grad4, grad3, sum2, grad4, grad4, g2, g2, grad3, grad4,
+        g2, g2, sum2, fa3, g2, g2, grad3, g2, grad4, g2, grad3, dW1a, g2, pair, grad3, g2, grad3, g2, pair, g2, S2a, grad4, dW2a, fa3, g2, grad3, g2,
+        S2b, sum3, dW2b, grad2, sum3, fa3, grad2, dW1b, sum3, grad1, grad3, fa3, grad1, grad2, fa3, pair, sum3, fs2, fa3, grad2, grad2, pair, grad1,
+        fa3, grad2, fs2, fa3, pair, grad2, grad1, grad1, fa3, fa3, fs2, grad1, fs2, grad1, fs2, pair, fs2, fa3, fs2, grad2, grad1, grad4, fs2, grad3,
+        fs2, fs2, grad4, fs2, grad2, fa3, grad1, fs2, grad1, fa3, grad2, fs2,
     )
 
 
-N_BATCHES = 60
-N_COPIES = 156
+N_BATCHES = 72
+N_COPIES = 192
 
 
 def step_call(x_tokens, dy_tokens, w_col, w_row, a_old, s_old, a_inv, s_inv, scale):
@@ -682,9 +756,9 @@
     hbm = pl.BlockSpec(memory_space=pl.ANY)
     scratch = [pltpu.VMEM((2,) + tall, bf16), pltpu.VMEM((2,) + wide, bf16)] + [pltpu.VMEM((WIDTH, WIDTH), bf16)] * 2 + [pltpu.VMEM(cube + (PIECE, WIDTH), bf16)] * 3
     scratch += [pltpu.VMEM(tall, bf16)] * 5 + [pltpu.VMEM(wide, bf16)] * 2 + [pltpu.VMEM((2,) + wide, bf16), pltpu.VMEM(wide, bf16)]
-    scratch += [pltpu.VMEM((4, SIDE, CORES, PIECE, TRI * BLOCK), f32), pltpu.VMEM((4, SIDE, PIECE, TRI * BLOCK), f32), pltpu.VMEM((4, 3, PIECE, TRI * BLOCK), f32)]
+    scratch += [pltpu.VMEM((SIDE, SIDE, CORES, PIECE, TRI * BLOCK), f32), pltpu.VMEM((SIDE, SIDE, PIECE, TRI * BLOCK), f32), pltpu.VMEM((4, 3, PIECE, TRI * BLOCK), f32)]
     scratch += [pltpu.VMEM((4, PIECE, TRI * BLOCK), f32), pltpu.VMEM((4, PIECE, FACTOR_COLS), f32)]
-    scratch += [pltpu.VMEM((2, SIDE, CORES, PIECE, GRAD_COLS), f32), pltpu.VMEM((4, SIDE, PIECE, GRAD_COLS), f32), pltpu.VMEM((4, 3, PIECE, GRAD_COLS), f32)]
+    scratch += [pltpu.VMEM((2, SIDE, CORES, PIECE, GRAD_COLS), f32), pltpu.VMEM((SIDE, SIDE, PIECE, GRAD_COLS), f32), pltpu.VMEM((4, 3, PIECE, GRAD_COLS), f32)]
     scratch += [pltpu.VMEM((4, 2, PIECE, GRAD_COLS), f32), pltpu.VMEM((4, rows, HALF + BLOCK), f32), pltpu.VMEM((2, 256, HALF), f32)]
     scratch += [pltpu.SemaphoreType.DMA((num,)) for num in (16, 6, 2, N_BATCHES, N_COPIES)]
     return pl.pallas_call(
@@ -698,7 +772,8 @@
     )(x_tokens, dy_tokens, w_col, w_row, a_old, s_old, a_inv, s_inv)
 
 
-def finish_kernel(scale, inv_rows, fact, grads, s_old_col, a_old_row, s_inv_col, a_inv_row, a_new, s_new, u_col, u_row, s_new_col, a_new_row, buf, turned, sums, u_col_buf, u_row_buf, load_sems, out_sems, turn_sems, small_sems):
+def finish_kernel(scale, inv_rows, fact, grads, s_old_col, a_old_row, s_inv_col, a_inv_row, a_new, s_new, u_col, u_row, s_new_col, a_new_row, buf, turned, sums, u_col_buf, u_row_buf, load_sems, out_sems, turn_sems, far_sems, far_out_sems, small_sems):
+    mid = PLANE // CORES
     outs = [(a_new, 0), (s_new, 1), (a_new, 1), (s_new, 0)]
 
     def load(mat, row):
@@ -706,7 +781,13 @@
         return pltpu.make_async_copy(fact.at[z, y, :, :, mat], buf.at[mat, row], load_sems.at[mat * PLANE + row])
 
     def turn_done(slot):
-        return pltpu.make_async_copy(turned.at[slot], turned.at[slot], turn_sems.at[slot])
+        ref = turned.at[slot, pl.ds(0, TRI - 2)]
+        return pltpu.make_async_copy(ref, ref, turn_sems.at[slot])
+
+    def far_done(row):
+        slot = lax.rem(row, CORES)
+        ref = turned.at[slot, TRI - 2]
+        return pltpu.make_async_copy(ref, ref, far_sems.at[slot])
 
     def start_load(mat):
         def body(row, carry):
@@ -716,13 +797,13 @@
 
     load_sums = pltpu.make_async_copy(grads, sums, out_sems.at[4])
     load_sums.start()
-    for mat in range(4):
+    for mat in range(SIDE):
         start_load(mat)
     half = HALF
 
     def new_blocks():
         load_sums.wait()
-        for layer in range(4):
+        for layer in range(SIDE):
             block, num = scale * sums[layer, :, 0, :, half:].reshape(BLOCK, BLOCK), 1 - layer // 2
             if layer % 2 == 1:
                 s_new_col[num] = FACTOR_DECAY * s_old_col[num] + block
@@ -747,29 +828,46 @@
     for mat, (out, num) in enumerate(outs):
         def row_step(row, carry):
             load(mat, row).wait()
-            slot = lax.rem(row, 2)
+            slot = lax.rem(row, CORES)
             if mat in (1, 2):
-                @pl.when(row < PLANE // 2)
+                @pl.when(row < mid)
                 def _():
                     small_product(2 * mat - 2, row)
 
-                @pl.when(row >= PLANE // 2)
+                @pl.when(row >= mid)
                 def _():
-                    small_product(2 * mat - 1, row - PLANE // 2)
-            for j in range(TRI):
+                    small_product(2 * mat - 1, row - mid)
+            far = TRI - 1
+            def place_block(j, sem):
                 cols = span_of(lax.rem(row + j, PLANE), BLOCK)
-                pltpu.make_async_copy(buf.at[mat, row, :, :, :, pl.ds(j * BLOCK, BLOCK)], out.at[num, row, :, :, :, cols], out_sems.at[mat]).start()
+                pltpu.make_async_copy(buf.at[mat, row, :, :, :, pl.ds(j * BLOCK, BLOCK)], out.at[num, row, :, :, :, cols], sem).start()
+
+            def place_turned(j, sem):
+                block = buf[mat, row, :, :, :, j * BLOCK:(j + 1) * BLOCK].reshape(BLOCK, BLOCK).T
+                turned[slot, j - 1] = block.reshape(SIDE, CORES, PIECE, BLOCK)
+                pltpu.make_async_copy(turned.at[slot, j - 1], out.at[num, lax.rem(row + j, PLANE), :, :, :, span_of(row, BLOCK)], sem).start()
+
+            for j in range(far):
+                place_block(j, out_sems.at[mat])
             if mat > 0:
                 turn_done(slot).wait()
             else:
                 @pl.when(row >= 2)
                 def _():
                     turn_done(slot).wait()
-            for j in range(1, TRI - 1):
-                other = lax.rem(row + j, PLANE)
-                block = buf[mat, row, :, :, :, j * BLOCK:(j + 1) * BLOCK].reshape(BLOCK, BLOCK).T
-                turned[slot, j - 1] = block.reshape(SIDE, CORES, PIECE, BLOCK)
-                pltpu.make_async_copy(turned.at[slot, j - 1], out.at[num, other, :, :, :, span_of(row, BLOCK)], turn_sems.at[slot]).start()
+            for j in range(1, far):
+                place_turned(j, turn_sems.at[slot])
+
+            @pl.when(row < mid)
+            def _():
+                if mat > 0:
+                    far_done(row).wait()
+                else:
+                    @pl.when(row >= 2)
+                    def _():
+                        far_done(row).wait()
+                place_block(far, far_out_sems.at[mat])
+                place_turned(far, far_sems.at[slot])
             return carry
 
         if mat == 1:
@@ -778,13 +876,16 @@
         if mat in (1, 2):
             for move in move_small(mat - 1):
                 move.start()
-    for batch in range(2):
+    for batch in range(CORES):
         for move in move_small(batch):
             move.wait()
-    for slot in range(2):
+    for slot in range(CORES):
         turn_done(slot).wait()
-    for mat in range(4):
-        pltpu.make_async_copy(buf.at[mat], buf.at[mat], out_sems.at[mat]).wait()
+        far_done(slot).wait()
+    for mat in range(SIDE):
+        near, far = buf.at[mat, :, :, :, :, pl.ds(0, mid * BLOCK)], buf.at[mat, pl.ds(0, mid), :, :, :, pl.ds(0, BLOCK)]
+        pltpu.make_async_copy(near, near, out_sems.at[mat]).wait()
+        pltpu.make_async_copy(far, far, far_out_sems.at[mat]).wait()
 
 
 def finish_call(fact, grads, s_old_col, a_old_row, s_inv_col, a_inv_row, scale, inv_rows):
@@ -796,7 +897,7 @@
         out_shape=[jax.ShapeDtypeStruct(shape, f32) for shape in shapes],
         in_specs=[hbm] * 2 + [vmem] * 4,
         out_specs=[hbm] * 4 + [vmem] * 2,
-        scratch_shapes=[pltpu.VMEM((4, PLANE, SIDE, CORES, PIECE, FACTOR_COLS), f32), pltpu.VMEM((2, TRI - 2, SIDE, CORES, PIECE, BLOCK), f32), pltpu.VMEM(grads.shape, f32), pltpu.VMEM((2, WIDTH, BLOCK), f32), pltpu.VMEM((2, BLOCK, WIDTH), f32)] + [pltpu.SemaphoreType.DMA((num,)) for num in (4 * PLANE, 5, 2, 4)],
+        scratch_shapes=[pltpu.VMEM((4, PLANE, SIDE, CORES, PIECE, FACTOR_COLS), f32), pltpu.VMEM((2, TRI - 1, SIDE, CORES, PIECE, BLOCK), f32), pltpu.VMEM(grads.shape, f32), pltpu.VMEM((2, WIDTH, BLOCK), f32), pltpu.VMEM((2, BLOCK, WIDTH), f32)] + [pltpu.SemaphoreType.DMA((num,)) for num in (SIDE * PLANE, 5, CORES, CORES, SIDE, SIDE)],
         compiler_params=pltpu.CompilerParams(vmem_limit_bytes=67043328),
         name='finish',
     )(fact, grads, s_old_col, a_old_row, s_inv_col, a_inv_row)

time: 258 us -> 254 us (0.984)
  Pallas kernels: 257 us -> 253 us
    pallas_call x1, Pallas kernels: 218 us -> 214 us  [step_call(): pl.pallas_call(functools.partial(step_kernel, scale), out_shape=[jax.Shap...]
where the time goes in v3:
time: 254 us
  Pallas kernels  253 us (100%)
    pallas_call x1, Pallas kernels, step_call(): pl.pallas_call(functools.partial(step_kernel, scale), out_shape=[jax.Shap...  214 us
    pallas_call x1, Pallas kernels, finish_call(): pl.pallas_call(functools.partial(finish_kernel, scale, inv_rows), out_sha...  39.3 us

profile of v3, /device:TPU:1, one launch (start us, length us, event | category | flops | bytes accessed | tf_op | source)
XLA Modules:
  0.0 253.7 jit_solution(16256530561747100749)
XLA Ops:
  0.6 213.5 %step.1 = (f32[4,4,4,2,4,16,1152]{6,5,4,3,2,1,0:T(8,128)}, f32[4,4,2,32,1152]{4,3,2,1,0:T(8,128)}) custom-call(bf16[2048,2048]{1,0:T(8,128)(2,1)} %x_hbm.1, bf16[2048,2048]{1,0:T(8,128)(2,1)} %dy_hbm.1, bf16[2,2048,128]{2,1,0:T(8,128)(2,1)} %w_col_hbm.1, bf16[2,128,2048]{2,1,0:T(8,128)(2,1)} %w_row_hbm.1, f32[2,2048,2048]{2,1,0:T(8,128)} %a_old.1, ...), custom_call_target="tpu_custom_call" | custom-call | tf_op jit(solution)/shard_map/step/pallas_call | solution.py:764
  214.2 39.3 %finish.1 = (f32[2,16,4,2,16,2048]{5,4,3,2,1,0:T(8,128)}, f32[2,16,4,2,16,2048]{5,4,3,2,1,0:T(8,128)}, f32[2,2048,128]{2,1,0:T(8,128)}, f32[2,128,2048]{2,1,0:T(...) custom-call(f32[4,4,4,2,4,16,1152]{6,5,4,3,2,1,0:T(8,128)} %get-tuple-element.14.fact, ...), custom_call_target="tpu_custom_call" | custom-call | tf_op jit(solution)/shard_map/finish/pallas_call | solution.py:895

commit v4 on v3

--- a/solution.py
+++ b/solution.py
@@ -136,9 +136,8 @@
 
     def pass_on(order, k):
         copies.wait(batch, ('b', order, k), like(4))
-        for step, part in ((-1, low), (1, high)) if k != 2 else ((1, whole),):
+        for step, part in ((-1, low), (1, high)):
             send(order, ('end', k), (k, step), part, 0, -step)
-        for step in BOTH_WAYS:
             on_piece(order, *steps(order, k, step))
 
     for order in ORDERS:
@@ -722,25 +721,25 @@
 
 
 W_TWO_CUTS = (0, 640, 1408, 2048)
-W_THREE_CUTS = (0, 896, 1920, 2048)
+W_THREE_CUTS = (0, 640, 1920, 2048)
 PAIR_CUTS = (0, 384, 896, 1024)
 LATE_CUTS = (0, 512, 640, 1024)
-W_TWO_WAYS = (-1, 1, 2)
-W_THREE_WAYS = (-1, 0)
-PAIR_WAYS = (0, 1)
+W_TWO_WAYS = ()
+W_THREE_WAYS = ()
+PAIR_WAYS = (-1, 0)
 LATE_WAYS = ()
 MOSTLY_X = (('y', 'z', 'x'), ('z', 'y', 'x'), ('x', 'y', 'z'))
 
 
 def plan(w2, w3, h2, g2, pair, fa3, fs2, sum0, sum1, sum2, sum3, grad4, grad3, grad2, grad1, z0, z1, swap, z2, back, A1, S4, A3, S2a, S2b, dW4, dW3, dW2a, dW2b, dW1a, dW1b, t3):
     return (
-        w2, w2, z0, w3, w2, z1, w2, A1, sum0, w2, S4, sum1, swap, sum0, sum1, w2, t3, t3, t3, w2, sum0, sum1, w2, w3, t3, w2, sum0, w2, w2, sum1, w2,
-        pair, w2, w3, z2, h2, pair, h2, w3, h2, w3, h2, pair, h2, h2, h2, h2, w3, h2, h2, h2, h2, h2, h2, pair, w3, h2, w3, h2, w3, w3, pair, h2, w3,
-        w3, pair, pair, A3, w3, back, g2, dW3, sum2, g2, dW4, grad4, grad3, grad4, g2, sum2, grad4, grad3, sum2, grad4, grad4, g2, g2, grad3, grad4,
-        g2, g2, sum2, fa3, g2, g2, grad3, g2, grad4, g2, grad3, dW1a, g2, pair, grad3, g2, grad3, g2, pair, g2, S2a, grad4, dW2a, fa3, g2, grad3, g2,
-        S2b, sum3, dW2b, grad2, sum3, fa3, grad2, dW1b, sum3, grad1, grad3, fa3, grad1, grad2, fa3, pair, sum3, fs2, fa3, grad2, grad2, pair, grad1,
-        fa3, grad2, fs2, fa3, pair, grad2, grad1, grad1, fa3, fa3, fs2, grad1, fs2, grad1, fs2, pair, fs2, fa3, fs2, grad2, grad1, grad4, fs2, grad3,
-        fs2, fs2, grad4, fs2, grad2, fa3, grad1, fs2, grad1, fa3, grad2, fs2,
+        w2, w2, z0, w3, z1, w2, A1, S4, sum0, w2, swap, sum0, sum1, w2, t3, t3, t3, t3, sum1, sum0, w2, sum1, sum0, w3, sum1, pair, w2, w2, w2, w3,
+        w2, w3, w2, pair, w2, w2, w3, z2, h2, w3, h2, h2, w3, h2, w3, h2, w3, h2, h2, h2, h2, h2, h2, pair, h2, h2, h2, w3, h2, h2, h2, w3, pair,
+        pair, dW4, w3, pair, w3, back, g2, grad4, dW3, grad3, grad4, A3, sum2, grad3, g2, g2, sum2, grad4, g2, grad3, g2, grad4, g2, sum2, pair,
+        grad4, grad4, sum2, g2, g2, pair, grad3, g2, fa3, grad3, grad4, g2, g2, grad3, dW1a, grad3, g2, g2, pair, dW2a, fa3, S2a, g2, grad4, g2, g2,
+        grad3, g2, S2b, dW2b, sum3, fa3, grad2, dW1b, grad1, sum3, grad2, grad1, sum3, grad2, fa3, sum3, fs2, fa3, fa3, grad3, fa3, pair, grad1,
+        grad2, grad2, fs2, grad2, fa3, grad1, fa3, grad3, grad1, fa3, pair, grad2, fs2, grad1, fs2, grad1, fs2, fs2, pair, fa3, fs2, fa3, grad2,
+        grad1, grad4, fs2, grad2, fs2, fs2, grad4, fs2, grad1, pair, fa3, fs2, grad2, grad1, fs2,
     )
 
 

time: 254 us -> 249 us (0.980)
  Pallas kernels: 253 us -> 248 us
    pallas_call x1, Pallas kernels: 214 us -> 208 us  [step_call(): pl.pallas_call(functools.partial(step_kernel, scale), out_shape=[jax.Shap...]
where the time goes in v4:
time: 249 us
  Pallas kernels  248 us (100%)
    pallas_call x1, Pallas kernels, step_call(): pl.pallas_call(functools.partial(step_kernel, scale), out_shape=[jax.Shap...  208 us
    pallas_call x1, Pallas kernels, finish_call(): pl.pallas_call(functools.partial(finish_kernel, scale, inv_rows), out_sha...  39.3 us

profile of v4, /device:TPU:1, one launch (start us, length us, event | category | flops | bytes accessed | tf_op | source)
XLA Modules:
  0.0 248.5 jit_solution(17412428938719036197)
XLA Ops:
  0.6 208.4 %step.1 = (f32[4,4,4,2,4,16,1152]{6,5,4,3,2,1,0:T(8,128)}, f32[4,4,2,32,1152]{4,3,2,1,0:T(8,128)}) custom-call(bf16[2048,2048]{1,0:T(8,128)(2,1)} %x_hbm.1, bf16[2048,2048]{1,0:T(8,128)(2,1)} %dy_hbm.1, bf16[2,2048,128]{2,1,0:T(8,128)(2,1)} %w_col_hbm.1, bf16[2,128,2048]{2,1,0:T(8,128)(2,1)} %w_row_hbm.1, f32[2,2048,2048]{2,1,0:T(8,128)} %a_old.1, ...), custom_call_target="tpu_custom_call" | custom-call | tf_op jit(solution)/shard_map/step/pallas_call | solution.py:763
  209.0 39.3 %finish.1 = (f32[2,16,4,2,16,2048]{5,4,3,2,1,0:T(8,128)}, f32[2,16,4,2,16,2048]{5,4,3,2,1,0:T(8,128)}, f32[2,2048,128]{2,1,0:T(8,128)}, f32[2,128,2048]{2,1,0:T(...) custom-call(f32[4,4,4,2,4,16,1152]{6,5,4,3,2,1,0:T(8,128)} %get-tuple-element.14.fact, ...), custom_call_target="tpu_custom_call" | custom-call | tf_op jit(solution)/shard_map/finish/pallas_call | solution.py:894

commit v5 on v4

--- a/solution.py
+++ b/solution.py
@@ -187,20 +187,18 @@
     yield
     copies.wait((batch, 'near'), ONLY, near)
     near[across] = near[across] + src[across, core]
-    copies.start((batch, 'half'), 1, near.at[across, low], far.at[0, low], place.device('x', 1))
-    copies.start((batch, 'half'), -1, near.at[across, high], far.at[0, high], place.device('x', -1))
+    copies.start((batch, 'half'), ONLY, near.at[across, low], far.at[0, low], place.device('x', 1))
+    copies.start((batch, 'half'), ONLY, near.at[across, high], far.at[0, high], place.device('x', -1))
     for there in (right, left, here):
         near[there] = near[there] + src[there, core]
     yield
-    copies.wait((batch, 'half'), 1, far.at[0, low])
+    copies.wait((batch, 'half'), ONLY, far.at[0])
     near[right, low] = near[right, low] + far[0, low]
-    copies.start((batch, 'full'), 1, near.at[right], far.at[1], place.device('x', 1))
-    copies.wait((batch, 'half'), -1, far.at[0, high])
+    copies.start((batch, 'full'), ONLY, near.at[right], far.at[1], place.device('x', 1))
     near[left, high] = near[left, high] + far[0, high]
-    copies.start((batch, 'full'), -1, near.at[left], far.at[2], place.device('x', -1))
-    yield
-    copies.wait((batch, 'full'), 1, far.at[1])
-    copies.wait((batch, 'full'), -1, far.at[2])
+    copies.start((batch, 'full'), ONLY, near.at[left], far.at[2], place.device('x', -1))
+    yield
+    copies.wait((batch, 'full'), ONLY, far.at[pl.ds(1, 2)])
     store(near[here] + far[1] + far[2])
     copies.left((batch, 'near'), near)
     copies.left((batch, 'half'), far.at[0])
@@ -217,16 +215,15 @@
         copies.start((batch, 'hand'), ONLY, ref, ref, place.mate)
 
     for step in BOTH_WAYS:
-        copies.start((batch, 'all'), step, here, here, place.device('x', step))
+        copies.start((batch, 'all'), ONLY, here, here, place.device('x', step))
     hand(here)
     yield
+    copies.wait((batch, 'all'), ONLY, out.at[pl.ds(0, 2), 0])
     for step, ref, span in ((1, left, pl.ds(0, half)), (-1, right, pl.ds(half, half))):
-        copies.wait((batch, 'all'), step, ref)
-        copies.start((batch, 'all'), 2 * step, ref.at[span], ref.at[span], place.device('x', step))
+        copies.start((batch, 'all'), 'end', ref.at[span], ref.at[span], place.device('x', step))
         hand(ref)
     yield
-    for step, span in ((1, pl.ds(0, half)), (-1, pl.ds(half, half))):
-        copies.wait((batch, 'all'), 2 * step, across.at[span])
+    copies.wait((batch, 'all'), 'end', out.at[0, 0])
     hand(across)
     yield
     copies.wait((batch, 'hand'), ONLY, out.at[:, 0])
@@ -726,25 +723,25 @@
 LATE_CUTS = (0, 512, 640, 1024)
 W_TWO_WAYS = ()
 W_THREE_WAYS = ()
-PAIR_WAYS = (-1, 0)
+PAIR_WAYS = (2,)
 LATE_WAYS = ()
 MOSTLY_X = (('y', 'z', 'x'), ('z', 'y', 'x'), ('x', 'y', 'z'))
 
 
 def plan(w2, w3, h2, g2, pair, fa3, fs2, sum0, sum1, sum2, sum3, grad4, grad3, grad2, grad1, z0, z1, swap, z2, back, A1, S4, A3, S2a, S2b, dW4, dW3, dW2a, dW2b, dW1a, dW1b, t3):
     return (
-        w2, w2, z0, w3, z1, w2, A1, S4, sum0, w2, swap, sum0, sum1, w2, t3, t3, t3, t3, sum1, sum0, w2, sum1, sum0, w3, sum1, pair, w2, w2, w2, w3,
-        w2, w3, w2, pair, w2, w2, w3, z2, h2, w3, h2, h2, w3, h2, w3, h2, w3, h2, h2, h2, h2, h2, h2, pair, h2, h2, h2, w3, h2, h2, h2, w3, pair,
-        pair, dW4, w3, pair, w3, back, g2, grad4, dW3, grad3, grad4, A3, sum2, grad3, g2, g2, sum2, grad4, g2, grad3, g2, grad4, g2, sum2, pair,
-        grad4, grad4, sum2, g2, g2, pair, grad3, g2, fa3, grad3, grad4, g2, g2, grad3, dW1a, grad3, g2, g2, pair, dW2a, fa3, S2a, g2, grad4, g2, g2,
-        grad3, g2, S2b, dW2b, sum3, fa3, grad2, dW1b, grad1, sum3, grad2, grad1, sum3, grad2, fa3, sum3, fs2, fa3, fa3, grad3, fa3, pair, grad1,
-        grad2, grad2, fs2, grad2, fa3, grad1, fa3, grad3, grad1, fa3, pair, grad2, fs2, grad1, fs2, grad1, fs2, fs2, pair, fa3, fs2, fa3, grad2,
-        grad1, grad4, fs2, grad2, fs2, fs2, grad4, fs2, grad1, pair, fa3, fs2, grad2, grad1, fs2,
+        w2, z0, w2, z1, w3, A1, w2, S4, sum0, t3, t3, sum1, w2, sum0, sum1, swap, w2, sum0, sum1, t3, w3, sum0, sum1, pair, w2, w2, w2, w2, t3, w3,
+        w2, w3, pair, w2, w2, w3, w2, z2, h2, h2, w3, h2, w3, h2, w3, pair, h2, h2, h2, w3, h2, h2, h2, w3, w3, w3, h2, h2, w3, h2, h2, h2, h2, h2,
+        pair, A3, dW4, pair, sum2, back, g2, grad4, dW3, grad3, grad4, g2, sum2, g2, grad3, grad4, sum2, pair, g2, grad4, grad4, g2, grad4, grad3,
+        sum2, g2, grad4, pair, g2, grad3, g2, g2, grad3, fa3, g2, grad4, grad3, grad3, g2, g2, pair, dW2a, S2a, pair, g2, g2, dW1a, fa3, pair, g2,
+        grad3, g2, g2, S2b, sum3, pair, sum3, fa3, dW2b, grad2, sum3, dW1b, grad1, grad2, fa3, grad1, sum3, grad3, fs2, grad2, fa3, grad1, grad3,
+        fs2, fa3, grad2, grad2, fa3, grad2, fa3, grad4, grad1, grad1, grad2, fs2, grad1, fs2, grad1, fa3, fa3, fs2, fa3, fa3, grad2, fs2, fs2, grad1,
+        pair, fs2, fs2, fa3, fs2, fs2, grad2, grad4, pair, grad1, fs2, grad2, grad1, fs2,
     )
 
 
 N_BATCHES = 72
-N_COPIES = 192
+N_COPIES = 168
 
 
 def step_call(x_tokens, dy_tokens, w_col, w_row, a_old, s_old, a_inv, s_inv, scale):

time: 249 us -> 249 us (level)
  no operation moved by 1% of the time
where the time goes in v5:
time: 249 us; the launch traced here: 248 us
  Pallas kernels  247 us (99%)
    pallas_call x1, Pallas kernels, step_call(): pl.pallas_call(functools.partial(step_kernel, scale), out_shape=[jax.Shap...  208 us
    pallas_call x1, Pallas kernels, finish_call(): pl.pallas_call(functools.partial(finish_kernel, scale, inv_rows), out_sha...  39.3 us

profile of v5, /device:TPU:1, one launch (start us, length us, event | category | flops | bytes accessed | tf_op | source)
XLA Modules:
  0.0 248.2 jit_solution(16143705606088049630)
XLA Ops:
  0.6 208.1 %step.1 = (f32[4,4,4,2,4,16,1152]{6,5,4,3,2,1,0:T(8,128)}, f32[4,4,2,32,1152]{4,3,2,1,0:T(8,128)}) custom-call(bf16[2048,2048]{1,0:T(8,128)(2,1)} %x_hbm.1, bf16[2048,2048]{1,0:T(8,128)(2,1)} %dy_hbm.1, bf16[2,2048,128]{2,1,0:T(8,128)(2,1)} %w_col_hbm.1, bf16[2,128,2048]{2,1,0:T(8,128)(2,1)} %w_row_hbm.1, f32[2,2048,2048]{2,1,0:T(8,128)} %a_old.1, ...), custom_call_target="tpu_custom_call" | custom-call | tf_op jit(solution)/shard_map/step/pallas_call | solution.py:760
  208.7 39.3 %finish.1 = (f32[2,16,4,2,16,2048]{5,4,3,2,1,0:T(8,128)}, f32[2,16,4,2,16,2048]{5,4,3,2,1,0:T(8,128)}, f32[2,2048,128]{2,1,0:T(8,128)}, f32[2,128,2048]{2,1,0:T(...) custom-call(f32[4,4,4,2,4,16,1152]{6,5,4,3,2,1,0:T(8,128)} %get-tuple-element.14.fact, ...), custom_call_target="tpu_custom_call" | custom-call | tf_op jit(solution)/shard_map/finish/pallas_call | solution.py:891
